TPU v7x, 32 devices: a whole 2x2x4 slice. The times are simulated.
32 devices in a mesh: row: 4 (over z), col: 8 (over y, x, core).
Axes of the slice: x: 2, y: 2, z: 4, core: 2. Of those that a mesh axis runs over, the one named last changes fastest.
Arguments:
- cell_index: int32 [2, 3, 65536], P(None, None, ('row', 'col')), may hold values from 0 to 255, as said below
- fraction: float32 [2, 3, 65536], P(None, None, ('row', 'col')), may hold values from 0 to 1
- charge: float32 [2, 65536], P(None, ('row', 'col')), may hold values from -4 to 4
- atom_count: int32 [2, 32], P(None, ('row', 'col')), may hold values from 1024 to 2048, as said below
- influence: float32 [256, 256, 256], P('row', 'col'), as said below
Outputs:
- forces: float32 [2, 3, 65536], P(None, None, ('row', 'col'))
Inputs may be any that keep to these rules, and one draw needn't show every extreme that they name: `cell_index`: slot a belongs to pencil p = a // 2048; with P = 8, its first cell index lies in [(p // P) * 64, (p // P + 1) * 64) and its second in [(p % P) * 32, (p % P + 1) * 32). `atom_count`: in every frame some pencil has all 2048 slots live. Even: influence[a, b, c] equals influence[(-a) mod 256, (-b) mod 256, (-c) mod 256]; it is 0 at the root and positive elsewhere.
All inputs are finite; a program needn't handle non-finite values.
Results may differ from a plain program's by a relative error of at most 0.0003.
Values sent between devices are 32-bit elements; how exact they have to be, the bound alone decides.
A program may use at most 128 MiB of HBM per device.

v0:
```python
import functools
import math

import jax
import jax.numpy as jnp
from jax import lax
from jax.experimental import pallas as pl
from jax.experimental.pallas import tpu as pltpu
from jax.sharding import PartitionSpec as P

PRECISION = lax.Precision.HIGH


def shifted(shard, axis, by):
    count = lax.axis_size(axis)
    return lax.ppermute(shard, axis, [(i, (i + by) % count) for i in range(count)])


def contract(form, left, right):
    return jnp.einsum(form, left, right, precision=PRECISION, preferred_element_type=jnp.float32)


def dft_tables(length):
    counter = jnp.arange(length, dtype=jnp.int32)
    product = counter[:, None] * counter[None, :] % length
    angle = product.astype(jnp.float32) * (2.0 * math.pi / length)
    return (jnp.cos(angle), jnp.sin(angle))


def spline_lists(fraction):
    nothing = jnp.zeros_like(fraction)
    levels = [fraction, 1.0 - fraction]
    slopes = levels
    for degree in range(3, 7):
        padded = levels + [nothing]
        following = []
        for offset in range(degree):
            beneath = padded[offset - 1] if offset > 0 else nothing
            following.append(
                ((fraction + offset) * padded[offset] + (degree - fraction - offset) * beneath)
                * (1.0 / (degree - 1))
            )
        if degree == 6:
            slopes = [
                padded[offset] - (padded[offset - 1] if offset > 0 else nothing)
                for offset in range(6)
            ]
        levels = following
    return levels, slopes


def dense_rows(anchor, weight_rows, extent, wrapped):
    positions = lax.broadcasted_iota(jnp.int32, (extent, anchor.shape[1]), 0)
    distance = anchor - positions
    if wrapped:
        distance = jnp.where(distance < 0, distance + extent, distance)
    matrices = [jnp.zeros(positions.shape, jnp.float32) for _ in weight_rows]
    for offset in range(6):
        hit = distance == offset
        matrices = [
            jnp.where(hit, weights[offset], matrix)
            for weights, matrix in zip(weight_rows, matrices)
        ]
    return matrices


def halves_of(value):
    high = value.astype(jnp.bfloat16)
    low = (value - high.astype(jnp.float32)).astype(jnp.bfloat16)
    return high, low


def rows_of(lists, dimension):
    return [row[dimension : dimension + 1, :] for row in lists]


def spread_kernel(
    rows_padded, cols_padded, anchors_ref, fraction_ref, charge_ref, mesh_ref, first_ref, high_ref, low_ref
):
    length = mesh_ref.shape[2]
    values, unused = spline_lists(fraction_ref[0])
    anchors = anchors_ref[0]
    (first,) = dense_rows(anchors[0:1], [rows_of(values, 0)], rows_padded, False)
    first_ref[...] = first * charge_ref[0]
    (second,) = dense_rows(anchors[1:2], [rows_of(values, 1)], cols_padded, False)
    (third,) = dense_rows(anchors[2:3], [rows_of(values, 2)], length, True)
    high_ref[...], low_ref[...] = halves_of(third)

    @pl.when(pl.program_id(1) == 0)
    def clear():
        mesh_ref[...] = jnp.zeros_like(mesh_ref)

    chunk = 8 * cols_padded
    form = (((1,), (1,)), ((), ()))

    @pl.loop(0, rows_padded // 8)
    def add_rows(part):
        first_rows = first_ref[pl.ds(pl.multiple_of(part * 8, 8), 8), :]
        product = first_rows[:, None, :] * second[None, :, :]
        high, low = halves_of(product.reshape(chunk, product.shape[2]))
        third_high = high_ref[...]
        total = lax.dot_general(high, third_high, form, preferred_element_type=jnp.float32)
        total += lax.dot_general(low, third_high, form, preferred_element_type=jnp.float32)
        total += lax.dot_general(high, low_ref[...], form, preferred_element_type=jnp.float32)
        mesh_ref[0, pl.ds(pl.multiple_of(part * chunk, 8), chunk), :] += total


def force_kernel(
    rows_padded,
    cols_padded,
    anchors_ref,
    fraction_ref,
    charge_ref,
    field_high_ref,
    field_low_ref,
    force_ref,
    first_ref,
    first_slope_ref,
    third_ref,
):
    length = field_high_ref.shape[2]
    values, slopes = spline_lists(fraction_ref[0])
    anchors = anchors_ref[0]
    size = anchors.shape[1]
    first_ref[...], first_slope_ref[...] = dense_rows(
        anchors[0:1], [rows_of(values, 0), rows_of(slopes, 0)], rows_padded, False
    )
    second, second_slope = dense_rows(
        anchors[1:2], [rows_of(values, 1), rows_of(slopes, 1)], cols_padded, False
    )
    third, third_slope = dense_rows(
        anchors[2:3], [rows_of(values, 2), rows_of(slopes, 2)], length, True
    )
    third_ref[0], third_ref[1] = halves_of(third)
    third_ref[2], third_ref[3] = halves_of(third_slope)
    chunk = 8 * cols_padded

    def add_rows(part, sums):
        rows = pl.ds(pl.multiple_of(part * 8, 8), 8)
        lines = pl.ds(pl.multiple_of(part * chunk, 16), chunk)
        high, low = field_high_ref[0, lines, :], field_low_ref[0, lines, :]

        def sampled(place):
            total = jnp.dot(high, third_ref[place], preferred_element_type=jnp.float32)
            total += jnp.dot(low, third_ref[place], preferred_element_type=jnp.float32)
            total += jnp.dot(high, third_ref[place + 1], preferred_element_type=jnp.float32)
            return total.reshape(8, cols_padded, size)

        plain = sampled(0)
        along = jnp.sum(plain * second[None], axis=1) * first_slope_ref[rows, :]
        weights = first_ref[rows, :]
        across = jnp.sum(plain * second_slope[None], axis=1) * weights
        sloped = sampled(2)
        upward = jnp.sum(sloped * second[None], axis=1) * weights
        return (sums[0] + along, sums[1] + across, sums[2] + upward)

    nothing = jnp.zeros((8, size), jnp.float32)
    sums = lax.fori_loop(0, rows_padded // 8, add_rows, (nothing, nothing, nothing))
    for dimension in range(3):
        total = jnp.sum(sums[dimension], axis=0, keepdims=True)
        force_ref[0, dimension : dimension + 1, :] = -charge_ref[0] * total


def atom_specs(size):
    return [
        pl.BlockSpec((1, 3, size), lambda step, group: (step, 0, group)),
        pl.BlockSpec((1, 3, size), lambda step, group: (step, 0, group)),
        pl.BlockSpec((1, 1, size), lambda step, group: (step, 0, group)),
    ]


def spread(anchors, fraction, charges, rows_padded, cols_padded, length, size):
    steps_count, unused, atoms_local = fraction.shape
    lines = rows_padded * cols_padded
    return pl.pallas_call(
        functools.partial(spread_kernel, rows_padded, cols_padded),
        grid=(steps_count, atoms_local // size),
        in_specs=atom_specs(size),
        out_specs=pl.BlockSpec((1, lines, length), lambda step, group: (step, 0, 0)),
        out_shape=jax.ShapeDtypeStruct((steps_count, lines, length), jnp.float32),
        scratch_shapes=[
            pltpu.VMEM((rows_padded, size), jnp.float32),
            pltpu.VMEM((length, size), jnp.bfloat16),
            pltpu.VMEM((length, size), jnp.bfloat16),
        ],
        compiler_params=pltpu.CompilerParams(vmem_limit_bytes=48 * 1024 * 1024),
        name="spread",
    )(anchors, fraction, charges)


def sample(anchors, fraction, charges, field, rows_padded, cols_padded, size):
    steps_count, unused, atoms_local = fraction.shape
    lines, length = field.shape[1:]
    leading = lax.reduce_precision(field, exponent_bits=8, mantissa_bits=7)
    high, low = leading.astype(jnp.bfloat16), (field - leading).astype(jnp.bfloat16)
    field_spec = pl.BlockSpec((1, lines, length), lambda step, group: (step, 0, 0))
    return pl.pallas_call(
        functools.partial(force_kernel, rows_padded, cols_padded),
        grid=(steps_count, atoms_local // size),
        in_specs=atom_specs(size) + [field_spec, field_spec],
        out_specs=pl.BlockSpec((1, 3, size), lambda step, group: (step, 0, group)),
        out_shape=jax.ShapeDtypeStruct((steps_count, 3, atoms_local), jnp.float32),
        scratch_shapes=[
            pltpu.VMEM((rows_padded, size), jnp.float32),
            pltpu.VMEM((rows_padded, size), jnp.float32),
            pltpu.VMEM((4, length, size), jnp.bfloat16),
        ],
        compiler_params=pltpu.CompilerParams(vmem_limit_bytes=48 * 1024 * 1024),
        name="sample",
    )(anchors, fraction, charges, high, low)


def along_rows(meshes, offset):
    return shifted(meshes, "row", offset)


def along_columns(meshes, offset):
    return shifted(meshes, "col", offset)


def across_columns(halves):
    return (
        lax.all_to_all(halves[0], "col", split_axis=2, concat_axis=2, tiled=True),
        lax.all_to_all(halves[1], "col", split_axis=2, concat_axis=2, tiled=True),
    )


def fold_rims(meshes, block_rows, block_cols):
    incoming = along_rows(meshes[:, :5], -1)
    meshes = meshes.at[:, block_rows : block_rows + 5].add(incoming)
    interior = meshes[:, 5:]
    incoming = along_columns(interior[:, :, :5], -1)
    interior = interior.at[:, :, block_cols : block_cols + 5].add(incoming)
    return interior[:, :, 5:]


def extend_rims(fields, block_rows, block_cols):
    incoming = along_columns(fields[:, :, block_cols - 5 :], 1)
    widened = jnp.concatenate([incoming, fields], axis=2)
    incoming = along_rows(widened[:, block_rows - 5 :], 1)
    return jnp.concatenate([incoming, widened], axis=1)


def forward_transform(real_part, imag_part, cosines, sine_table, cols_count):
    batch_size, block_rows, block_cols, length = real_part.shape
    first_part = contract("sxyz,zk->sxky", real_part, cosines) + contract(
        "sxyz,zk->sxky", imag_part, sine_table
    )
    second_part = contract("sxyz,zk->sxky", imag_part, cosines) - contract(
        "sxyz,zk->sxky", real_part, sine_table
    )
    first_part = first_part.reshape(batch_size, block_rows, length * block_cols)
    second_part = second_part.reshape(batch_size, block_rows, length * block_cols)
    first_part, second_part = across_columns((first_part, second_part))
    slab_depth = length // cols_count
    first_part = first_part.reshape(batch_size, block_rows, cols_count, slab_depth, block_cols)
    second_part = second_part.reshape(batch_size, block_rows, cols_count, slab_depth, block_cols)
    column_cosines = cosines.reshape(cols_count, block_cols, length)
    column_sines = sine_table.reshape(cols_count, block_cols, length)
    third_part = contract("sxcky,cyv->sxvk", first_part, column_cosines) + contract(
        "sxcky,cyv->sxvk", second_part, column_sines
    )
    fourth_part = contract("sxcky,cyv->sxvk", second_part, column_cosines) - contract(
        "sxcky,cyv->sxvk", first_part, column_sines
    )
    third_part = third_part.reshape(batch_size, block_rows, length * slab_depth)
    fourth_part = fourth_part.reshape(batch_size, block_rows, length * slab_depth)
    third_part, fourth_part = (
        lax.all_to_all(third_part, "row", split_axis=2, concat_axis=1, tiled=True),
        lax.all_to_all(fourth_part, "row", split_axis=2, concat_axis=1, tiled=True),
    )
    fifth_part = contract("sxj,xw->sjw", third_part, cosines) + contract(
        "sxj,xw->sjw", fourth_part, sine_table
    )
    sixth_part = contract("sxj,xw->sjw", fourth_part, cosines) - contract(
        "sxj,xw->sjw", third_part, sine_table
    )
    return (fifth_part, sixth_part)


def inverse_transform(real_part, imag_part, cosines, sine_table, rows_count, cols_count):
    batch_size, mode_rows, length = real_part.shape
    first_part = contract("sjw,wx->sxj", real_part, cosines) - contract(
        "sjw,wx->sxj", imag_part, sine_table
    )
    second_part = contract("sjw,wx->sxj", imag_part, cosines) + contract(
        "sjw,wx->sxj", real_part, sine_table
    )
    first_part, second_part = (
        lax.all_to_all(first_part, "row", split_axis=1, concat_axis=2, tiled=True),
        lax.all_to_all(second_part, "row", split_axis=1, concat_axis=2, tiled=True),
    )
    block_rows = length // rows_count
    block_cols = length // cols_count
    slab_depth = length // cols_count
    first_part = first_part.reshape(batch_size, block_rows, length, slab_depth)
    second_part = second_part.reshape(batch_size, block_rows, length, slab_depth)
    column_cosines = cosines.reshape(length, cols_count, block_cols)
    column_sines = sine_table.reshape(length, cols_count, block_cols)
    third_part = contract("sxvk,vcy->sxcky", first_part, column_cosines) - contract(
        "sxvk,vcy->sxcky", second_part, column_sines
    )
    fourth_part = contract("sxvk,vcy->sxcky", second_part, column_cosines) + contract(
        "sxvk,vcy->sxcky", first_part, column_sines
    )
    third_part = third_part.reshape(batch_size, block_rows, length * block_cols)
    fourth_part = fourth_part.reshape(batch_size, block_rows, length * block_cols)
    third_part, fourth_part = across_columns((third_part, fourth_part))
    third_part = third_part.reshape(batch_size, block_rows, length, block_cols)
    fourth_part = fourth_part.reshape(batch_size, block_rows, length, block_cols)
    real_out = contract("sxky,kz->sxyz", third_part, cosines) - contract(
        "sxky,kz->sxyz", fourth_part, sine_table
    )
    imag_out = contract("sxky,kz->sxyz", fourth_part, cosines) + contract(
        "sxky,kz->sxyz", third_part, sine_table
    )
    return (real_out, imag_out)


def shards(cell_index, fraction, charge, atom_count, influence):
    rows_count = lax.axis_size("row")
    cols_count = lax.axis_size("col")
    row_place = lax.axis_index("row")
    col_place = lax.axis_index("col")
    length = influence.shape[2]
    block_rows = length // rows_count
    block_cols = length // cols_count
    rows_padded = -(-(block_rows + 5) // 8) * 8
    cols_padded = -(-(block_cols + 5) // 8) * 8
    atoms_local = charge.shape[1]
    size = math.gcd(256, atoms_local)
    cosines, sine_table = dft_tables(length)
    normalizer = 1.0 / float(length) ** 3
    green_local = influence.reshape(-1, length) * normalizer
    slot_ids = jnp.arange(atoms_local, dtype=jnp.int32)

    origin = jnp.stack([row_place * block_rows - 5, col_place * block_cols - 5, 0])
    anchors = cell_index - origin[None, :, None]
    charges = jnp.where(slot_ids[None, :] < atom_count, charge, 0.0)[:, None, :]
    meshes = spread(anchors, fraction, charges, rows_padded, cols_padded, length, size)
    meshes = meshes.reshape(-1, rows_padded, cols_padded, length)
    meshes = meshes[:, : block_rows + 5, : block_cols + 5]
    charge_mesh = fold_rims(meshes, block_rows, block_cols)
    mode_real, mode_imag = forward_transform(
        charge_mesh[0::2], charge_mesh[1::2], cosines, sine_table, cols_count
    )
    even_part, odd_part = inverse_transform(
        mode_real * green_local,
        mode_imag * green_local,
        cosines,
        sine_table,
        rows_count,
        cols_count,
    )
    potential = jnp.stack([even_part, odd_part], axis=1).reshape(charge_mesh.shape)
    extended = extend_rims(potential, block_rows, block_cols)
    extended = jnp.pad(
        extended,
        ((0, 0), (0, rows_padded - block_rows - 5), (0, cols_padded - block_cols - 5), (0, 0)),
    ).reshape(-1, rows_padded * cols_padded, length)
    return sample(anchors, fraction, charges, extended, rows_padded, cols_padded, size)


def solution(mesh):
    placed = (
        P(None, None, ("row", "col")),
        P(None, None, ("row", "col")),
        P(None, ("row", "col")),
        P(None, ("row", "col")),
        P("row", "col", None),
    )
    return jax.shard_map(
        shards, mesh=mesh, in_specs=placed, out_specs=P(None, None, ("row", "col")), check_vma=False
    )
```

profile of v0, /device:TPU:0, one launch (start us, length us, event | category | flops | bytes accessed | tf_op | source)
XLA Modules:
  0.0 849.8 jit_solution(13613648852195129827)
XLA Ops:
  2.6 52.7 %spread.1 = f32[2,2880,256]{2,1,0:T(8,128)S(1)} custom-call(s32[2,3,2048]{2,1,0:T(4,128)S(1)} %copy_subtract_fusion.anchors_ref, f32[2,3,2048]{2,1,0:T(4,128)S(1)} %copy.114.fraction_ref, f32[2,1,2048]{2,1,0:T(1,128)S(1)} %broadcast_in_dim.7.charge_ref), custom_call_target="tpu_custom_call" | custom-call | tf_op jit(solution)/shard_map/spread/pallas_call | solution.py:175
  71.1 7.3 collective-permute-done.1
  87.8 38.5 %reduce.6 = f32[8192,64]{1,0:T(8,128)} reduce(f32[8192,1,64]{2,1,0:T(1,128)} %bitcast.226, f32[]{:T(128)} %broadcast.618), dimensions={1}, to_apply=%bitcast.180.reduce_sub_computation | reduce | bytes 4194308
  126.2 7.2 reshape.441
  149.9 38.4 %reduce.4 = f32[8192,64]{1,0:T(8,128)} reduce(f32[8192,1,64]{2,1,0:T(1,128)} %bitcast.227, f32[]{:T(128)} %broadcast.618), dimensions={1}, to_apply=%bitcast.178.reduce_sub_computation | reduce | bytes 4194308
  200.0 7.2 reduce.7
  214.4 12.2 %all-to-all-done.1 = f32[8,1,65536]{2,1,0:T(1,128)} async-done(((f32[8,1,65536]{2,1,0:T(1,128)}), f32[8,1,65536]{2,1,0:T(1,128)}, u32[]{:S(2)}, u32[]{:S(2)}) %all-to-all-start.1) | async-done | bytes 2097184 | tf_op jit(solution)/shard_map/all_to_all | solution.py:224
  226.6 7.4 reduce.5
  257.2 38.4 %reduce.10 = f32[8192,64]{1,0:T(8,128)} reduce(f32[8192,1,64]{2,1,0:T(1,128)} %bitcast.228, f32[]{:T(128)} %broadcast.618), dimensions={1}, to_apply=%bitcast.184.reduce_sub_computation | reduce | bytes 4194308
  324.8 38.4 %reduce.8 = f32[8192,64]{1,0:T(8,128)} reduce(f32[8192,1,64]{2,1,0:T(1,128)} %bitcast.229, f32[]{:T(128)} %broadcast.618), dimensions={1}, to_apply=%bitcast.182.reduce_sub_computation | reduce | bytes 4194308
  378.8 7.7 reduce.11
  404.1 16.6 %all-to-all-done.3 = f32[4,1,131072]{2,1,0:T(1,128)} async-done(((f32[4,1,131072]{2,1,0:T(1,128)}), f32[4,1,131072]{2,1,0:T(1,128)}, u32[]{:S(2)}, u32[]{:S(2)}) %all-to-all-start.3) | async-done | bytes 2097184 | tf_op jit(solution)/shard_map/all_to_all | solution.py:270
  420.7 7.7 reduce.9
  428.4 7.4 reshape.444
  474.8 37.1 %all-to-all-done.4 = f32[1,256,2048]{2,0,1:T(1,128)} async-done(((f32[1,256,2048]{2,0,1:T(1,128)}), f32[1,256,2048]{2,0,1:T(1,128)}, u32[]{:S(2)}, u32[]{:S(2)}) %all-to-all-start.4) | async-done | bytes 2097184 | tf_op jit(solution)/shard_map/all_to_all | solution.py:290
  532.2 32.3 %all-to-all-done.5 = f32[1,256,2048]{2,0,1:T(1,128)} async-done(((f32[1,256,2048]{2,0,1:T(1,128)}), f32[1,256,2048]{2,0,1:T(1,128)}, u32[]{:S(2)}, u32[]{:S(2)}) %all-to-all-start.5) | async-done | bytes 2097184 | tf_op jit(solution)/shard_map/all_to_all | solution.py:291
  575.7 8.0 convolution_subtract_fusion.2
  583.7 38.4 %reduce.14 = f32[8192,64]{1,0:T(8,128)} reduce(f32[8192,1,64]{2,1,0:T(1,128)} %bitcast.219, f32[]{:T(128)} %broadcast.618), dimensions={1}, to_apply=%bitcast.188.reduce_sub_computation | reduce | bytes 4194308
  644.3 38.4 %reduce.12 = f32[8192,64]{1,0:T(8,128)} reduce(f32[8192,1,64]{2,1,0:T(1,128)} %bitcast.218, f32[]{:T(128)} %broadcast.618), dimensions={1}, to_apply=%bitcast.186.reduce_sub_computation | reduce | bytes 4194308
  721.1 8.6 %reduce.13 = f32[8,65536]{1,0:T(8,128)} reduce(f32[8,1,65536]{2,1,0:T(1,128)} %all-to-all-done.7, f32[]{:T(128)} %broadcast.618), dimensions={1}, to_apply=%all_to_all.71.reduce_sub_computation | reduce | bytes 4194308 | tf_op jit(solution)/shard_map/all_to_all | solution.py:224
  729.6 9.0 %reshape.448 = f32[8192,1,64]{2,1,0:T(1,128)} reshape(f32[8,65536]{1,0:T(8,128)} %reduce.13) | data formatting | bytes 4194304
  752.5 10.9 %collective-permute-done.2 = f32[2,64,5,256]{3,1,2,0:T(8,128)S(1)} collective-permute-done((f32[2,64,5,256]{3,1,2,0:T(8,128)S(1)}, f32[2,64,5,256]{3,1,2,0:T(8,128)S(1)}, u32[]{:S(2)}, u32[]{:S(2)}) %collective-permute-start.2) | collective-permute-done | bytes 655392 | tf_op jit(solution)/shard_map/ppermute | solution.py:16
  764.0 10.4 %collective-permute-done.3 = f32[2,5,37,256]{3,2,1,0:T(8,128)S(1)} collective-permute-done((f32[2,5,37,256]{3,2,1,0:T(8,128)S(1)}, f32[2,5,37,256]{3,2,1,0:T(8,128)S(1)}, u32[]{:S(2)}, u32[]{:S(2)}) %collective-permute-start.3) | collective-permute-done | bytes 378912 | tf_op jit(solution)/shard_map/ppermute | solution.py:16
  776.6 72.1 %sample.1 = f32[2,3,2048]{2,1,0:T(4,128)S(1)} custom-call(s32[2,3,2048]{2,1,0:T(4,128)S(1)} %copy_subtract_fusion.anchors_ref, f32[2,3,2048]{2,1,0:T(4,128)S(1)} %copy.114.fraction_ref, f32[2,1,2048]{2,1,0:T(1,128)S(1)} %broadcast_in_dim.7.charge_ref, bf16[2,2880,256]{2,1,0:T(8,128)(2,1)S(1)} %get-tuple-element.30.field_high_ref, ...), custom_call_target="tpu_custom_call" | custom-call | tf_op jit(solution)/shard_map/sample/pallas_call | solution.py:197
  (112 shorter events, 296.5 us)
Async XLA Ops:
  55.6 13.2 %collective-permute-start = (f32[2,5,37,256]{3,0,2,1:T(2,128)S(1)}, f32[2,5,37,256]{3,0,2,1:T(2,128)S(1)}, u32[]{:S(2)}, u32[]{:S(2)}) collective-permute-start(f32[2,5,37,256]{3,0,2,1:T(2,128)S(1)} %copy.126), channel_id=1, source_target_pairs={{0,24},{8,0},{16,8},{24,16},{1,25},{9,1},{17,9},{25,17},{2,26},{10... | collective-permute-start | bytes 1136648 | tf_op jit(solution)/shard_map/ppermute | solution.py:16
  69.0 9.4 %collective-permute-start.1 = (f32[2,64,5,256]{3,1,2,0:T(8,128)S(1)}, f32[2,64,5,256]{3,1,2,0:T(8,128)S(1)}, u32[]{:S(2)}, u32[]{:S(2)}) collective-permute-start(f32[2,64,5,256]{3,1,2,0:T(8,128)S(1)} %slice.106), channel_id=1, source_target_pairs={{0,7},{1,0},{2,1},{3,2},{4,3},{5,4},{6,5},{7,6},{8,15},{9,8},{10,9... | collective-permute-start | bytes 1966088 | tf_op jit(solution)/shard_map/ppermute | solution.py:16
  78.5 2.2 copy-start.2
  133.5 62.0 %all-to-all-start = ((f32[8,1,65536]{2,1,0:T(1,128)}), f32[8,1,65536]{2,1,0:T(1,128)}, u32[]{:S(2)}, u32[]{:S(2)}) async-start(f32[8,1,65536]{2,1,0:T(1,128)} %reshape.441), calls=%async_computation | async-start | bytes 4194304 | tf_op jit(solution)/shard_map/all_to_all | solution.py:223
  195.5 31.1 %all-to-all-start.1 = ((f32[8,1,65536]{2,1,0:T(1,128)}), f32[8,1,65536]{2,1,0:T(1,128)}, u32[]{:S(2)}, u32[]{:S(2)}) async-start(f32[8,1,65536]{2,1,0:T(1,128)} %reshape.439), calls=%async_computation.1 | async-start | bytes 4194304 | tf_op jit(solution)/shard_map/all_to_all | solution.py:224
  241.2 7.1 copy-start.1
  301.1 67.6 %all-to-all-start.2 = ((f32[4,1,131072]{2,1,0:T(1,128)}), f32[4,1,131072]{2,1,0:T(1,128)S(1)}, u32[]{:S(2)}, u32[]{:S(2)}) async-start(f32[4,1,131072]{2,1,0:T(1,128)} %reshape.445), calls=%async_computation.2 | async-start | bytes 4194304 | tf_op jit(solution)/shard_map/all_to_all | solution.py:269
  306.9 6.7 copy-start
  368.7 1.4 copy-start.9
  370.1 50.6 %all-to-all-start.3 = ((f32[4,1,131072]{2,1,0:T(1,128)}), f32[4,1,131072]{2,1,0:T(1,128)}, u32[]{:S(2)}, u32[]{:S(2)}) async-start(f32[4,1,131072]{2,1,0:T(1,128)} %reshape.443), calls=%async_computation.3 | async-start | bytes 4194304 | tf_op jit(solution)/shard_map/all_to_all | solution.py:270
  398.7 1.3 copy-start.5
  440.8 2.7 copy-start.7
  440.8 2.7 copy-start.10
  446.3 2.8 copy-start.6
  451.8 1.3 copy-start.4
  459.6 52.3 %all-to-all-start.4 = ((f32[1,256,2048]{2,0,1:T(1,128)}), f32[1,256,2048]{2,0,1:T(1,128)}, u32[]{:S(2)}, u32[]{:S(2)}) async-start(f32[1,256,2048]{2,0,1:T(1,128)} %copy.98), calls=%async_computation.4 | async-start | bytes 4194304 | tf_op jit(solution)/shard_map/all_to_all | solution.py:290
  511.9 52.5 %all-to-all-start.5 = ((f32[1,256,2048]{2,0,1:T(1,128)}), f32[1,256,2048]{2,0,1:T(1,128)}, u32[]{:S(2)}, u32[]{:S(2)}) async-start(f32[1,256,2048]{2,0,1:T(1,128)} %copy.101), calls=%async_computation.5 | async-start | bytes 4194304 | tf_op jit(solution)/shard_map/all_to_all | solution.py:291
  629.3 60.6 %all-to-all-start.6 = ((f32[8,1,65536]{2,1,0:T(1,128)}), f32[8,1,65536]{2,1,0:T(1,128)}, u32[]{:S(2)}, u32[]{:S(2)}) async-start(f32[8,1,65536]{2,1,0:T(1,128)} %reshape.449), calls=%async_computation.6 | async-start | bytes 4194304 | tf_op jit(solution)/shard_map/all_to_all | solution.py:223
  689.9 31.2 %all-to-all-start.7 = ((f32[8,1,65536]{2,1,0:T(1,128)}), f32[8,1,65536]{2,1,0:T(1,128)}, u32[]{:S(2)}, u32[]{:S(2)}) async-start(f32[8,1,65536]{2,1,0:T(1,128)} %reshape.447), calls=%async_computation.7 | async-start | bytes 4194304 | tf_op jit(solution)/shard_map/all_to_all | solution.py:224
  743.8 3.7 copy-start.3
  743.8 3.7 copy-start.8
  752.5 11.0 %collective-permute-start.2 = (f32[2,64,5,256]{3,1,2,0:T(8,128)S(1)}, f32[2,64,5,256]{3,1,2,0:T(8,128)S(1)}, u32[]{:S(2)}, u32[]{:S(2)}) collective-permute-start(f32[2,64,5,256]{3,1,2,0:T(8,128)S(1)} %copy.112), channel_id=1, source_target_pairs={{0,1},{1,2},{2,3},{3,4},{4,5},{5,6},{6,7},{7,0},{8,9},{9,10},{10,1... | collective-permute-start | bytes 1966088 | tf_op jit(solution)/shard_map/ppermute | solution.py:16
  763.9 10.5 %collective-permute-start.3 = (f32[2,5,37,256]{3,2,1,0:T(8,128)S(1)}, f32[2,5,37,256]{3,2,1,0:T(8,128)S(1)}, u32[]{:S(2)}, u32[]{:S(2)}) collective-permute-start(f32[2,5,37,256]{3,2,1,0:T(8,128)S(1)} %pad_maximum_fusion), channel_id=1, source_target_pairs={{0,8},{8,16},{16,24},{24,0},{1,9},{9,17},{17,25},{25,1},{2,10},{10... | collective-permute-start | bytes 1136648 | tf_op jit(solution)/shard_map/ppermute | solution.py:16
where the time goes:
time: 856 us; the launch traced here: 850 us
  other arithmetic  284 us (33%)
  local copies, waits for them, and re-layouts  162 us (19%)
  waiting for transfers between devices  137 us (16%)
  Pallas kernels  125 us (15%)
  matrix products  94.4 us (11%)
  starting transfers between devices  45.8 us (5%)
    unnamed x6, other arithmetic  230 us
    dot_general x24, matrix products, contract(): jnp.einsum(form, left, right, precision=PRECISION, preferred_element_type...  94.4 us
    unnamed x38, local copies, waits for them, and re-layouts  92 us
    pallas_call x1, Pallas kernels, sample(): pl.pallas_call(functools.partial(force_kernel, rows_padded, cols_padded),...  72.1 us
    pallas_call x1, Pallas kernels, spread(): pl.pallas_call(functools.partial(spread_kernel, rows_padded, cols_padded)...  52.7 us
    all_to_all x1, waiting for transfers between devices, inverse_transform(): lax.all_to_all(first_part, 'row', split_axis=1, concat_axis=2, tiled=True)  37.1 us
    ppermute x4, waiting for transfers between devices, shifted(): lax.ppermute(shard, axis, [(i, (i + by) % count) for i in range(count)])  34.7 us
    all_to_all x1, waiting for transfers between devices, inverse_transform(): lax.all_to_all(second_part, 'row', split_axis=1, concat_axis=2, tiled=True)  32.3 us
  transfers between devices with their start and end apart: 12, of which 9 were waited for; matrix products, arithmetic and copies ran while one was open for 31% of the time, Pallas kernels for 0%

commit v1 on v0

v1 whole, which is shorter than its diff:
```python
import functools
import math

import jax
import jax.numpy as jnp
from jax import lax
from jax.experimental import pallas as pl
from jax.experimental.pallas import tpu as pltpu
from jax.sharding import PartitionSpec as P

MESH = pl.DeviceIdType.MESH
LANES = 128
CHUNK = 9
HALO = 8
NT = (((1,), (1,)), ((), ()))
NN = (((1,), (0,)), ((), ()))


def dot(left, right, form=NN):
    return lax.dot_general(left, right, form, preferred_element_type=jnp.float32)


def halves_of(value):
    high = value.astype(jnp.bfloat16)
    return high, (value - high.astype(jnp.float32)).astype(jnp.bfloat16)


def spline_rows(fraction):
    nothing = jnp.zeros_like(fraction)
    levels = [fraction, 1.0 - fraction]
    slopes = levels
    for degree in range(3, 7):
        padded = levels + [nothing]
        following = []
        for offset in range(degree):
            beneath = padded[offset - 1] if offset > 0 else nothing
            following.append(
                ((fraction + offset) * padded[offset] + (degree - fraction - offset) * beneath)
                * (1.0 / (degree - 1))
            )
        if degree == 6:
            slopes = [
                padded[offset] - (padded[offset - 1] if offset > 0 else nothing)
                for offset in range(6)
            ]
        levels = following
    return levels, slopes


def dense(distance, lists):
    results = [jnp.zeros(distance.shape, jnp.float32) for _ in lists]
    for offset in range(6):
        hit = distance == offset
        results = [jnp.where(hit, rows[offset], result) for rows, result in zip(lists, results)]
    return results


def row_of(lists, dimension):
    return [entry[dimension : dimension + 1, :] for entry in lists]


def phases(product, length):
    half = length // 2
    moved = product + half
    if length & (length - 1):
        turned = lax.rem(moved, length) - half
    else:
        turned = (moved & (length - 1)) - half
    angle = turned.astype(jnp.float32) * (2.0 * math.pi / length / 4.0)
    square = angle * angle
    sine = angle * (
        1.0
        + square
        * (-1.0 / 6 + square * (1.0 / 120 + square * (-1.0 / 5040 + square * (1.0 / 362880))))
    )
    cosine = 1.0 + square * (
        -0.5
        + square
        * (1.0 / 24 + square * (-1.0 / 720 + square * (1.0 / 40320 - square * (1.0 / 3628800))))
    )
    for _ in range(2):
        sine, cosine = 2.0 * sine * cosine, 1.0 - 2.0 * sine * sine
    return cosine, sine


def wave_rows(cosine, sine, cos_ref, sin_ref, rows):
    even = cos_ref[0] * rows[0]
    odd = sin_ref[0] * rows[0]
    for offset in range(1, 6):
        even += cos_ref[offset] * rows[offset]
        odd += sin_ref[offset] * rows[offset]
    return cosine * even + sine * odd


def sort_kernel(key_row_ref, key_col_ref, payload_ref, sorted_ref, rank_ref):
    atoms = key_row_ref.shape[2]

    @pl.loop(0, atoms // LANES)
    def count(part):
        lanes = pl.ds(pl.multiple_of(part * LANES, LANES), LANES)
        below = key_col_ref[0] < key_row_ref[0, :, lanes]
        rank_ref[0, :, lanes] = jnp.sum(jnp.where(below, 1.0, 0.0), axis=0, keepdims=True)

    value = payload_ref[0]
    first, rest = halves_of(value)
    left = value - first.astype(jnp.float32)
    third = (left - rest.astype(jnp.float32)).astype(jnp.bfloat16)
    pieces = jnp.concatenate([first, rest, third, jnp.zeros_like(first)], axis=0)
    rank = rank_ref[0].astype(jnp.int32)
    width = math.gcd(256, atoms)

    @pl.loop(0, atoms // width)
    def place(part):
        start = pl.multiple_of(part * width, width)
        spots = lax.broadcasted_iota(jnp.int32, (width, atoms), 0) + start
        chosen = jnp.where(rank == spots, 1.0, 0.0).astype(jnp.bfloat16)
        moved = dot(pieces, chosen, NT)
        sorted_ref[0, :, pl.ds(start, width)] = moved[0:8] + moved[8:16] + moved[16:24]


def sort_atoms(key_row, key_col, payload):
    frames, rows, atoms = payload.shape
    whole = lambda frame: (frame, 0, 0)
    return pl.pallas_call(
        sort_kernel,
        grid=(frames,),
        in_specs=[
            pl.BlockSpec((1, 1, atoms), whole),
            pl.BlockSpec((1, atoms, LANES), whole),
            pl.BlockSpec((1, rows, atoms), whole),
        ],
        out_specs=[pl.BlockSpec((1, rows, atoms), whole), pl.BlockSpec((1, 1, atoms), whole)],
        out_shape=[
            jax.ShapeDtypeStruct((frames, rows, atoms), jnp.float32),
            jax.ShapeDtypeStruct((frames, 1, atoms), jnp.float32),
        ],
        compiler_params=pltpu.CompilerParams(vmem_limit_bytes=32 * 1024 * 1024),
        name="sort_atoms",
    )(key_row, key_col, payload)


def unsort_kernel(rank_ref, force_ref, out_ref):
    atoms = rank_ref.shape[2]
    value = force_ref[0]
    high, low = halves_of(value)
    left = value - high.astype(jnp.float32)
    third = (left - low.astype(jnp.float32)).astype(jnp.bfloat16)
    pieces = jnp.concatenate([high, low, third, jnp.zeros_like(high)], axis=0)
    rank = rank_ref[0].astype(jnp.int32)
    width = math.gcd(256, atoms)

    @pl.loop(0, atoms // width)
    def place(part):
        start = pl.multiple_of(part * width, width)
        spots = lax.broadcasted_iota(jnp.int32, (atoms, width), 0)
        lanes = pl.ds(start, width)
        here = rank_ref[0, :, lanes].astype(jnp.int32)
        chosen = jnp.where(here == spots, 1.0, 0.0).astype(jnp.bfloat16)
        moved = dot(pieces, chosen, NN)
        out_ref[0, :, lanes] = moved[0:8] + moved[8:16] + moved[16:24]


def unsort_forces(rank, forces):
    frames, rows, atoms = forces.shape
    whole = lambda frame: (frame, 0, 0)
    return pl.pallas_call(
        unsort_kernel,
        grid=(frames,),
        in_specs=[pl.BlockSpec((1, 1, atoms), whole), pl.BlockSpec((1, rows, atoms), whole)],
        out_specs=pl.BlockSpec((1, rows, atoms), whole),
        out_shape=jax.ShapeDtypeStruct((frames, rows, atoms), jnp.float32),
        compiler_params=pltpu.CompilerParams(vmem_limit_bytes=32 * 1024 * 1024),
        name="unsort_forces",
    )(rank, forces)


class Layout:
    def __init__(self, frames, length, atoms):
        self.rows = lax.axis_size("row")
        self.cols = lax.axis_size("col")
        self.frames = frames
        self.length = length
        self.atoms = atoms
        self.group = self.rows // frames
        self.half_cols = self.cols // 2
        self.block_rows = length // self.rows
        self.block_cols = length // self.cols
        self.slots = length // 2 // (self.group * self.half_cols)
        self.own = self.slots // 2
        self.slots_padded = max(8, self.slots)
        self.wave_rows = 2 * self.slots_padded
        self.lines = self.half_cols * self.block_cols + HALO
        self.lines_padded = -(-(self.lines + CHUNK - 1) // 8) * 8
        self.splits = self.group // 2
        self.blocks = atoms // LANES
        self.span = self.block_rows + HALO


def gather_kernel(lay, mine_ref, all_ref, local_sem, send_sem, recv_sem, pass_sem, took_sem):
    row = lax.axis_index("row")
    col = lax.axis_index("col")
    pair = col // 2
    side = col % 2
    half = col // lay.half_cols
    place = col % lay.half_cols
    hub = half == side
    pair_start = (2 * pair) % lay.half_cols

    def first_send(frame, member):
        target = frame * lay.group + member
        index = frame * lay.group + member
        return target, pltpu.make_async_remote_copy(
            src_ref=mine_ref.at[frame],
            dst_ref=all_ref.at[row, place],
            send_sem=send_sem.at[index],
            recv_sem=recv_sem.at[row, side],
            device_id=(target, 2 * pair + half),
            device_id_type=MESH,
        )

    def self_copy(frame):
        return pltpu.make_async_copy(mine_ref.at[frame], all_ref.at[row, place], local_sem)

    for frame in range(lay.frames):
        for member in range(lay.group):
            target, copy = first_send(frame, member)
            alone = (target == row) & hub

            @pl.when(jnp.logical_not(alone))
            def send():
                copy.start()

            @pl.when(alone)
            def keep():
                self_copy(frame).start()

    def second_send(source, part, other):
        spot = pair_start + part
        return pltpu.make_async_remote_copy(
            src_ref=all_ref.at[source, spot],
            dst_ref=all_ref.at[source, spot],
            send_sem=pass_sem.at[source, part, other - 1],
            recv_sem=took_sem.at[source, spot],
            device_id=(row, 2 * ((pair + other) % lay.half_cols) + side),
            device_id_type=MESH,
        )

    def arrival(source, spot, sem):
        return pltpu.make_async_remote_copy(
            src_ref=all_ref.at[source, spot],
            dst_ref=all_ref.at[source, spot],
            send_sem=send_sem.at[0],
            recv_sem=sem,
            device_id=(row, col),
            device_id_type=MESH,
        )

    @pl.when(hub)
    def forward():
        for source in range(lay.rows):
            for part in range(2):
                spot = pair_start + part
                alone = (source == row) & (part == side)

                @pl.when(jnp.logical_not(alone))
                def landed():
                    arrival(source, spot, recv_sem.at[source, part]).wait_recv()

                @pl.when(alone)
                def kept():
                    self_copy(row // lay.group).wait()

                for other in range(1, lay.half_cols):
                    second_send(source, part, other).start()

    for frame in range(lay.frames):
        for member in range(lay.group):
            target, copy = first_send(frame, member)

            @pl.when(jnp.logical_not((target == row) & hub))
            def sent():
                copy.wait_send()

    for spot in range(lay.half_cols):
        local = hub & (pair == side * (lay.half_cols // 2) + spot // 2)

        @pl.when(jnp.logical_not(local))
        def took():
            for source in range(lay.rows):
                arrival(source, spot, took_sem.at[source, spot]).wait_recv()

    @pl.when(hub)
    def passed():
        for source in range(lay.rows):
            for part in range(2):
                for other in range(1, lay.half_cols):
                    second_send(source, part, other).wait_send()


def gather_atoms(lay, mine):
    frames, rows, atoms = mine.shape
    dma = pltpu.SemaphoreType.DMA
    return pl.pallas_call(
        functools.partial(gather_kernel, lay),
        in_specs=[pl.BlockSpec(memory_space=pltpu.VMEM)],
        out_specs=pl.BlockSpec(memory_space=pltpu.VMEM),
        out_shape=jax.ShapeDtypeStruct((lay.rows, lay.half_cols, rows, atoms), jnp.float32),
        scratch_shapes=[
            dma,
            dma((lay.rows,)),
            dma((lay.rows, 2)),
            dma((lay.rows, 2, lay.half_cols - 1)),
            dma((lay.rows, lay.half_cols)),
        ],
        compiler_params=pltpu.CompilerParams(has_side_effects=True),
        name="gather_atoms",
    )(mine)


def return_kernel(lay, force_ref, out_ref, local_sem, send_sem, recv_sem):
    row = lax.axis_index("row")
    col = lax.axis_index("col")
    side = col % 2
    frame = row // lay.group
    index = (row % lay.group) * lay.half_cols + col // 2
    copies = []
    for source in range(lay.rows):
        for spot in range(lay.half_cols):
            owner = side * lay.half_cols + spot
            copies.append(
                (
                    (source == row) & (owner == col),
                    pltpu.make_async_remote_copy(
                        src_ref=force_ref.at[source, spot],
                        dst_ref=out_ref.at[frame, index],
                        send_sem=send_sem.at[source, spot],
                        recv_sem=recv_sem.at[frame, index],
                        device_id=(source, owner),
                        device_id_type=MESH,
                    ),
                    pltpu.make_async_copy(
                        force_ref.at[source, spot], out_ref.at[frame, index], local_sem
                    ),
                )
            )
    for alone, copy, local in copies:

        @pl.when(jnp.logical_not(alone))
        def send():
            copy.start()

        @pl.when(alone)
        def keep():
            local.start()

    for alone, copy, local in copies:

        @pl.when(jnp.logical_not(alone))
        def sent():
            copy.wait_send()

        @pl.when(alone)
        def kept():
            local.wait()

    half = col // lay.half_cols
    for from_frame in range(lay.frames):
        for member in range(lay.group):
            for pair in range(lay.half_cols):
                slot = member * lay.half_cols + pair
                alone = (from_frame * lay.group + member == row) & (2 * pair + half == col)

                @pl.when(jnp.logical_not(alone))
                def landed():
                    pltpu.make_async_remote_copy(
                        src_ref=out_ref.at[from_frame, slot],
                        dst_ref=out_ref.at[from_frame, slot],
                        send_sem=send_sem.at[0, 0],
                        recv_sem=recv_sem.at[from_frame, slot],
                        device_id=(row, col),
                        device_id_type=MESH,
                    ).wait_recv()


def return_forces(lay, forces):
    rows, half_cols = forces.shape[:2]
    members = lay.group * half_cols
    dma = pltpu.SemaphoreType.DMA
    return pl.pallas_call(
        functools.partial(return_kernel, lay),
        in_specs=[pl.BlockSpec(memory_space=pltpu.VMEM)],
        out_specs=pl.BlockSpec(memory_space=pltpu.VMEM),
        out_shape=jax.ShapeDtypeStruct((lay.frames, members) + forces.shape[2:], jnp.float32),
        scratch_shapes=[dma, dma((rows, half_cols)), dma((lay.frames, members))],
        compiler_params=pltpu.CompilerParams(has_side_effects=True),
        name="return_forces",
    )(forces)


def atom_block(lay, atoms_ref, waves_ref, block, with_slopes):
    lanes = pl.ds(pl.multiple_of(block * LANES, LANES), LANES)
    piece = atoms_ref[0, 0, :, lanes]
    cells = piece[0:3].astype(jnp.int32)
    values, slopes = spline_rows(piece[3:6])
    charge = piece[6:7]
    spots = lax.broadcasted_iota(jnp.int32, (lay.span, LANES), 0)
    kinds = [values, slopes] if with_slopes else [values]
    wide = dense(cells[0:1] + HALO - spots, [row_of(kind, 0) for kind in kinds])
    pad = jnp.zeros((LANES - lay.span, LANES), jnp.float32)
    wide = [jnp.concatenate([entry, pad], axis=0) for entry in wide]
    cosine, sine = phases(waves_ref[0] * cells[2:3] + waves_ref[1], lay.length)
    return cells, kinds, charge, wide, cosine, sine


def line_weights(cells, kinds, start, lay):
    lines = lax.broadcasted_iota(jnp.int32, (-(-CHUNK // 8) * 8, LANES), 0) + start
    return dense(cells[1:2] + HALO - lines, [row_of(kind, 1) for kind in kinds])


def spread_kernel(lay, starts_ref, turns_ref, atoms_ref, waves_ref, cos_ref, sin_ref, mesh_ref):
    part = pl.program_id(1)
    pencil = pl.program_id(0) * lay.half_cols + part

    @pl.when(part == 0)
    def clear():
        mesh_ref[...] = jnp.zeros_like(mesh_ref)

    @pl.loop(0, lay.blocks)
    def add_block(block):
        turns = turns_ref[pencil * lay.blocks + block]

        @pl.when(turns > 0)
        def live():
            cells, kinds, charge, wide, cosine, sine = atom_block(
                lay, atoms_ref, waves_ref, block, False
            )
            waves = wave_rows(cosine, sine, cos_ref, sin_ref, row_of(kinds[0], 2)) * charge
            high, low = halves_of(wide[0])
            right = jnp.concatenate(
                [
                    jnp.concatenate([high, high], axis=1),
                    jnp.concatenate([low, low], axis=1),
                ],
                axis=0,
            )
            start = starts_ref[pencil * lay.blocks + block]

            @pl.loop(0, turns)
            def add_lines(turn):
                line = start + turn * CHUNK
                (weights,) = line_weights(cells, kinds, line, lay)
                product = jnp.concatenate(
                    [weights[i : i + 1] * waves for i in range(CHUNK)], axis=0
                )
                high, low = halves_of(product)
                total = dot(jnp.concatenate([high, low], axis=1), right, NT)
                where = pl.ds(pl.multiple_of(line * lay.wave_rows, lay.wave_rows), CHUNK * lay.wave_rows)
                mesh_ref[0, where, :] += total[:, :LANES] + total[:, LANES:]


def atom_specs(lay):
    fixed = lambda row, part, *refs: (0, 0, 0)
    return [
        pl.BlockSpec((1, 1, 8, lay.atoms), lambda row, part, *refs: (row, part, 0, 0)),
        pl.BlockSpec((2, lay.wave_rows, LANES), fixed),
        pl.BlockSpec((6, lay.wave_rows, LANES), fixed),
        pl.BlockSpec((6, lay.wave_rows, LANES), fixed),
    ]


def spread(lay, starts, turns, atoms, waves, cosines, sines):
    size = lay.lines_padded * lay.wave_rows
    return pl.pallas_call(
        functools.partial(spread_kernel, lay),
        grid_spec=pltpu.PrefetchScalarGridSpec(
            num_scalar_prefetch=2,
            grid=(lay.rows, lay.half_cols),
            in_specs=atom_specs(lay),
            out_specs=pl.BlockSpec((1, size, LANES), lambda row, part, *refs: (row, 0, 0)),
        ),
        out_shape=jax.ShapeDtypeStruct((lay.rows, size, LANES), jnp.float32),
        compiler_params=pltpu.CompilerParams(vmem_limit_bytes=40 * 1024 * 1024),
        cost_estimate=pl.CostEstimate(flops=10**10, bytes_accessed=10**7, transcendentals=0),
        name="spread",
    )(starts, turns, atoms, waves, cosines, sines)


def sample_kernel(
    lay, starts_ref, turns_ref, atoms_ref, waves_ref, cos_ref, sin_ref, high_ref, low_ref, out_ref
):
    pencil = pl.program_id(0) * lay.half_cols + pl.program_id(1)

    @pl.loop(0, lay.blocks)
    def sample_block(block):
        turns = turns_ref[pencil * lay.blocks + block]
        out_ref[0, 0, :, pl.ds(block, 1), :] = jnp.zeros((3, 1, LANES), jnp.float32)

        @pl.when(turns > 0)
        def live():
            cells, kinds, charge, wide, cosine, sine = atom_block(
                lay, atoms_ref, waves_ref, block, True
            )
            third = wave_rows(cosine, sine, cos_ref, sin_ref, row_of(kinds[0], 2))
            third_slope = wave_rows(cosine, sine, cos_ref, sin_ref, row_of(kinds[1], 2))
            both = jnp.concatenate(wide, axis=1)
            high, low = halves_of(both)
            right = jnp.concatenate([high, high], axis=0)
            start = starts_ref[pencil * lay.blocks + block]

            def add_lines(turn, sums):
                line = start + turn * CHUNK
                weights, weight_slopes = line_weights(cells, kinds, line, lay)
                where = pl.ds(pl.multiple_of(line * lay.wave_rows, lay.wave_rows), CHUNK * lay.wave_rows)
                field_high = high_ref[0, where, :]
                field = jnp.concatenate([field_high, low_ref[0, where, :]], axis=1)
                found = dot(field, right) + dot(field_high, low)
                plain, sloped, across = sums
                for i in range(CHUNK):
                    lines = slice(i * lay.wave_rows, (i + 1) * lay.wave_rows)
                    value = found[lines, :LANES]
                    plain += value * weights[i : i + 1]
                    across += value * weight_slopes[i : i + 1]
                    sloped += found[lines, LANES:] * weights[i : i + 1]
                return plain, sloped, across

            nothing = jnp.zeros((lay.wave_rows, LANES), jnp.float32)
            plain, sloped, across = lax.fori_loop(0, turns, add_lines, (nothing, nothing, nothing))
            for dimension, value in enumerate((sloped * third, across * third, plain * third_slope)):
                total = -charge * jnp.sum(value, axis=0, keepdims=True)
                out_ref[0, 0, dimension, pl.ds(block, 1), :] = total


def sample(lay, starts, turns, atoms, waves, cosines, sines, high, low):
    size = lay.lines_padded * lay.wave_rows
    field = pl.BlockSpec((1, size, LANES), lambda row, part, *refs: (row, 0, 0))
    shape = (lay.rows, lay.half_cols, 3, lay.blocks, LANES)
    return pl.pallas_call(
        functools.partial(sample_kernel, lay),
        grid_spec=pltpu.PrefetchScalarGridSpec(
            num_scalar_prefetch=2,
            grid=(lay.rows, lay.half_cols),
            in_specs=atom_specs(lay) + [field, field],
            out_specs=pl.BlockSpec((1, 1) + shape[2:], lambda row, part, *refs: (row, part, 0, 0, 0)),
        ),
        out_shape=jax.ShapeDtypeStruct(shape, jnp.float32),
        compiler_params=pltpu.CompilerParams(vmem_limit_bytes=40 * 1024 * 1024),
        cost_estimate=pl.CostEstimate(flops=10**10, bytes_accessed=10**7, transcendentals=0),
        name="sample",
    )(starts, turns, atoms, waves, cosines, sines, high, low)


def transform_kernel(
    lay,
    mesh_ref,
    green_ref,
    first_high,
    first_low,
    second_high,
    second_low,
    back_high,
    back_low,
    last_high,
    last_low,
    out_high,
    out_low,
    field_ref,
    mine_ref,
    send_ref,
    recv_ref,
    home_ref,
    extra_ref,
    send_sem,
    recv_sem,
    back_sem,
    home_sem,
):
    row = lax.axis_index("row")
    col = lax.axis_index("col")
    side = col % 2
    partner = (row, col + 1 - 2 * side)
    lines, length, own, padded = lay.lines, lay.length, lay.own, lay.slots_padded
    inner = lines - HALO

    def three(high, low, table_high, table_low):
        return dot(high, table_high) + dot(low, table_high) + dot(high, table_low)

    def push(index):
        return pltpu.make_async_remote_copy(
            src_ref=send_ref.at[index],
            dst_ref=recv_ref.at[index],
            send_sem=send_sem.at[index],
            recv_sem=recv_sem.at[index],
            device_id=partner,
            device_id_type=MESH,
        )

    def push_back(index):
        return pltpu.make_async_remote_copy(
            src_ref=send_ref.at[index],
            dst_ref=home_ref.at[index],
            send_sem=back_sem.at[index],
            recv_sem=home_sem.at[index],
            device_id=partner,
            device_id_type=MESH,
        )

    def forward(slot):
        rows = [
            jnp.concatenate(
                [mesh_ref[r, pl.ds(start, lines, stride=lay.wave_rows), :] for r in range(lay.rows)],
                axis=1,
            )
            for start in (slot, padded + slot)
        ]
        high, low = halves_of(jnp.concatenate(rows, axis=0))
        found = three(high, low, first_high[...], first_low[...])
        upper, lower = found[:lines], found[lines:]
        return upper[:, :length], upper[:, length:], lower[:, :length], lower[:, length:]

    for base, target in ((0, send_ref), (own, mine_ref)):
        away = base == 0

        @pl.loop(0, own)
        def first_pass(i):
            real_cos, real_sin, imag_cos, imag_sin = forward(base + i)

            @pl.when(i == 0)
            def mirrored():
                target[own, 0] = real_cos - imag_sin
                target[own, 1] = -imag_cos - real_sin

            target[i, 0] = real_cos + imag_sin
            target[i, 1] = imag_cos - real_sin
            if away:

                @pl.when(i == 0)
                def start_mirrored():
                    push(own).start()

                push(i).start()

    @pl.loop(0, own + 1)
    def sent(i):
        push(i).wait_send()

    number = message_number(lay, row, col)

    def spectrum(index):
        mine, other = mine_ref[index], recv_ref[index]
        parts = []
        for part in range(2):
            a, b = mine[part], other[part]
            parts.append(
                jnp.concatenate(
                    [
                        a[HALO:inner],
                        a[inner:] + b[:HALO],
                        b[HALO:inner],
                        b[inner:] + a[:HALO],
                    ],
                    axis=0,
                )
            )
        high, low = halves_of(jnp.concatenate(parts, axis=1))
        found = (
            dot(second_high[...], high) + dot(second_high[...], low) + dot(second_low[...], high)
        )
        cos_part, sin_part = found[:length], found[length:]
        real = cos_part[:, :length] + sin_part[:, length:]
        imag = cos_part[:, length:] - sin_part[:, :length]
        blocks = [green_ref[lax.rem(r + number, lay.rows), index] for r in range(lay.rows)]
        green = jnp.concatenate(blocks, axis=0)
        return real * green, imag * green

    push(own).wait_recv()
    extra_ref[0], extra_ref[1] = spectrum(own)

    @pl.loop(0, own)
    def second_pass(i):
        push(i).wait_recv()
        real, imag = spectrum(i)
        first = jnp.where(i == 0, 1.0, 0.0)
        real += first * extra_ref[0]
        imag += first * extra_ref[1]
        high, low = halves_of(jnp.concatenate([real, imag], axis=1))
        found = dot(back_high[...], high) + dot(back_high[...], low) + dot(back_low[...], high)
        cos_part, sin_part = found[: 2 * lines], found[2 * lines :]
        real = cos_part[:, :length] - sin_part[:, length:]
        imag = cos_part[:, length:] + sin_part[:, :length]
        mine_ref[i, 0] = real[:lines]
        mine_ref[i, 1] = imag[:lines]
        send_ref[i, 0] = real[lines:]
        send_ref[i, 1] = imag[lines:]
        push_back(i).start()

    cleared = 0 if lay.slots < padded else lines * lay.wave_rows
    total_rows = lay.lines_padded * lay.wave_rows
    for r in range(lay.rows):
        field_ref[r, pl.ds(cleared, total_rows - cleared), :] = jnp.zeros(
            (total_rows - cleared, LANES), jnp.float32
        )

    def last(local, planes_ref, i):
        high, low = halves_of(jnp.concatenate([planes_ref[i, 0], planes_ref[i, 1]], axis=1))
        found = three(high, low, last_high[...], last_low[...])
        for part in range(2):
            for r in range(lay.rows):
                lanes = (part * lay.rows + r) * LANES
                where = pl.ds(part * padded + local, lines, stride=lay.wave_rows)
                field_ref[r, where, :] = found[:, lanes : lanes + LANES]

    @pl.loop(0, own)
    def last_mine(i):
        last(own + i, mine_ref, i)

    @pl.loop(0, own)
    def last_home(i):
        push_back(i).wait_recv()
        last(i, home_ref, i)

    @pl.loop(0, lay.lines_padded)
    def split(line):
        where = pl.ds(pl.multiple_of(line * lay.wave_rows, lay.wave_rows), lay.wave_rows)
        for r in range(lay.rows):
            out_high[r, where, :], out_low[r, where, :] = halves_of(field_ref[r, where, :])

    @pl.loop(0, own)
    def returned(i):
        push_back(i).wait_send()


def message_number(lay, row, col):
    member = lax.rem(row, lay.group)
    frame = row // lay.group
    return (lax.rem(col, 2) * lay.frames + frame) * lay.splits + lax.rem(member, lay.splits)


def transform(lay, mesh, green, tables):
    dma = pltpu.SemaphoreType.DMA
    plane = (2, lay.lines, lay.length)
    vmem = pl.BlockSpec(memory_space=pltpu.VMEM)
    out = jax.ShapeDtypeStruct(mesh.shape, jnp.bfloat16)
    return pl.pallas_call(
        functools.partial(transform_kernel, lay),
        in_specs=[vmem] * (2 + len(tables)),
        out_specs=[vmem, vmem],
        out_shape=[out, out],
        scratch_shapes=[
            pltpu.VMEM(mesh.shape, jnp.float32),
            pltpu.VMEM((lay.own + 1,) + plane, jnp.float32),
            pltpu.VMEM((lay.own + 1,) + plane, jnp.float32),
            pltpu.VMEM((lay.own + 1,) + plane, jnp.float32),
            pltpu.VMEM((lay.own,) + plane, jnp.float32),
            pltpu.VMEM((2, lay.length, lay.length), jnp.float32),
            dma((lay.own + 1,)),
            dma((lay.own + 1,)),
            dma((lay.own,)),
            dma((lay.own,)),
        ],
        compiler_params=pltpu.CompilerParams(
            has_side_effects=True, vmem_limit_bytes=62 * 1024 * 1024
        ),
        cost_estimate=pl.CostEstimate(flops=10**10, bytes_accessed=10**7, transcendentals=0),
        name="transform",
    )(mesh, green, *tables)


def table_halves(value):
    leading = lax.reduce_precision(value, exponent_bits=8, mantissa_bits=7)
    return leading.astype(jnp.bfloat16), (value - leading).astype(jnp.bfloat16)


def make_tables(lay, side):
    length, half = lay.length, lay.half_cols * lay.block_cols
    waves = jnp.arange(length, dtype=jnp.int32)
    spots = jnp.arange(LANES, dtype=jnp.int32)
    blocks = jnp.arange(lay.rows, dtype=jnp.int32)
    zero = lax.optimization_barrier(jnp.int32(0))
    across = (blocks[:, None] * lay.block_rows + spots[None, :] - HALO).reshape(-1) + length + zero
    valid = jnp.tile(spots < lay.span, lay.rows)
    cosine, sine = phases(across[:, None] * waves[None, :], length)
    keep = valid[:, None]
    first = jnp.where(keep, jnp.concatenate([cosine, sine], axis=1), 0.0)
    cosine, sine = phases(across[None, :] * waves[:, None], length)
    top = jnp.concatenate([cosine, sine], axis=1)
    bottom = jnp.concatenate([-sine, cosine], axis=1)
    last = jnp.where(jnp.tile(valid, 2)[None, :], jnp.concatenate([top, bottom], axis=0), 0.0)
    along = waves + half * side
    second = jnp.concatenate(phases(waves[:, None] * along[None, :], length), axis=0)
    near = jnp.arange(lay.lines, dtype=jnp.int32) - HALO + length
    both = jnp.concatenate([near + half * side, near + half * (1 - side)])
    back = jnp.concatenate(phases(both[:, None] * waves[None, :], length), axis=0)
    tables = []
    for table in (first, second, back, last):
        tables.extend(table_halves(table))
    return tables


def make_waves(lay, row, col, side):
    length = lay.length
    member = row % lay.group
    source = 2 * (col // 2) + member // lay.splits
    split = member % lay.splits
    start = lay.block_cols * source + jnp.where(source >= lay.half_cols, 1, 0) + split * lay.slots
    index = jnp.arange(lay.slots_padded, dtype=jnp.int32)
    slot = jnp.where(index < lay.own, (1 - side) * lay.own, side * lay.own) + index % lay.own
    special = (source == 0) & (split == 0) & (slot == 0)
    waves = jnp.concatenate([start + slot, jnp.where(special, length // 2, start + slot)])
    turns = jnp.concatenate([jnp.zeros_like(slot), jnp.where(special, 0, length // 4)])
    live = jnp.tile(index < lay.slots, 2)[None, :, None]
    offsets = jnp.arange(6, dtype=jnp.int32)
    cosine, sine = phases(offsets[:, None] * waves[None, :], length)
    shape = (6, lay.wave_rows, LANES)
    cosines = jnp.broadcast_to(jnp.where(live, cosine[:, :, None], 0.0), shape)
    sines = jnp.broadcast_to(jnp.where(live, sine[:, :, None], 0.0), shape)
    both = jnp.broadcast_to(jnp.stack([waves, turns])[:, :, None], (2, lay.wave_rows, LANES))
    return both, cosines, sines


def share_green(lay, influence, row, col):
    length = lay.length
    rows, cols = lay.rows, lay.cols
    scale = 1.0 / float(length) ** 3
    used = lay.block_cols // 2
    offset = jnp.where(col >= lay.half_cols, 1, 0)
    middle = lax.ppermute(influence[:, 0, :], "col", [(lay.half_cols, 0)])
    block = lax.dynamic_slice_in_dim(influence, offset, used, axis=1).transpose(1, 0, 2)
    block = block.reshape(lay.splits, 2, lay.own, lay.block_rows, length)
    special = col == 0
    zeroth = block[0, 0, 0]
    extra = jnp.where(special, (0.5 * scale) * (zeroth - middle), 0.0)
    zeroth = jnp.where(special, (0.5 * scale) * (zeroth + middle), (2.0 * scale) * zeroth)
    block = jnp.concatenate([(2.0 * scale) * block, jnp.zeros_like(block[:, :, :1])], axis=2)
    block = block.at[0, 0, 0].set(zeroth).at[0, 0, lay.own].set(extra)
    block = block.reshape((2 * lay.splits,) + block.shape[2:])
    messages = []
    for number in range(rows):
        message = (number - row) % rows
        split = message % lay.splits
        side = message // (lay.frames * lay.splits)
        sent = lax.dynamic_index_in_dim(block, split * 2 + side, keepdims=False)
        pairs = []
        for r in range(rows):
            at = (number - r) % rows
            to_split, rest = at % lay.splits, at // lay.splits
            to_frame, to_side = rest % lay.frames, rest // lay.frames
            for c in range(cols):
                to_row = to_frame * lay.group + (c % 2) * lay.splits + to_split
                pairs.append((r * cols + c, to_row * cols + 2 * (c // 2) + to_side))
        messages.append(lax.ppermute(sent, ("row", "col"), pairs))
    return jnp.stack(messages)


def shards(cell_index, fraction, charge, atom_count, influence):
    frames, unused, atoms = fraction.shape
    lay = Layout(frames, influence.shape[2], atoms)
    row = lax.axis_index("row")
    col = lax.axis_index("col")
    side = col % 2
    green = share_green(lay, influence, row, col)
    tables = make_tables(lay, side)
    waves, cosines, sines = make_waves(lay, row, col, side)

    slot_ids = jnp.arange(atoms, dtype=jnp.int32)
    alive = slot_ids[None, :] < atom_count
    charges = jnp.where(alive, charge, 0.0)
    origin = jnp.stack([row * lay.block_rows, (col // lay.half_cols) * lay.half_cols * lay.block_cols, 0])
    cells = cell_index - origin[None, :, None]
    payload = jnp.concatenate(
        [
            cells.astype(jnp.float32),
            fraction,
            charges[:, None, :],
            alive[:, None, :].astype(jnp.float32),
        ],
        axis=1,
    )
    key = (jnp.where(alive, cells[:, 1], lay.length) * atoms + slot_ids[None, :]).astype(jnp.float32)
    key_col = jnp.broadcast_to(key[:, :, None], (frames, atoms, LANES))
    sorted_atoms, rank = sort_atoms(key[:, None, :], key_col, payload)
    shared = gather_atoms(lay, sorted_atoms)

    lines = shared[:, :, 1, :].reshape(lay.rows * lay.half_cols * lay.blocks, LANES)
    lives = shared[:, :, 7, :].reshape(lines.shape) > 0.5
    lowest = jnp.min(jnp.where(lives, lines, 1024.0), axis=1).astype(jnp.int32)
    highest = jnp.max(jnp.where(lives, lines, -1024.0), axis=1).astype(jnp.int32)
    starts = lowest + HALO - 5
    turns = jnp.where(highest >= lowest, (highest - lowest + 6 + CHUNK - 1) // CHUNK, 0)

    mesh = spread(lay, starts, turns, shared, waves, cosines, sines)
    high, low = transform(lay, mesh, green, tables)
    partial = sample(lay, starts, turns, shared, waves, cosines, sines, high, low)
    returned = return_forces(lay, partial)
    forces = jnp.sum(returned, axis=1).reshape(frames, 3, atoms)
    forces = jnp.pad(forces, ((0, 0), (0, 5), (0, 0)))
    return unsort_forces(rank, forces)[:, :3]


def solution(mesh):
    placed = (
        P(None, None, ("row", "col")),
        P(None, None, ("row", "col")),
        P(None, ("row", "col")),
        P(None, ("row", "col")),
        P("row", "col", None),
    )
    return jax.shard_map(
        shards, mesh=mesh, in_specs=placed, out_specs=P(None, None, ("row", "col")), check_vma=False
    )
```

time: 856 us -> 379 us (0.44)
  other arithmetic: 284 us -> 22.3 us
  Pallas kernels: 125 us -> 281 us
  local copies, waits for them, and re-layouts: 162 us -> 18 us
  waiting for transfers between devices: 137 us -> 41.1 us
  matrix products: 94.4 us -> 0 us
  starting transfers between devices: 45.8 us -> 16.3 us
    unnamed x6 -> x0, other arithmetic: 230 us -> none
    pallas_call x2 -> x7, Pallas kernels: 125 us -> 281 us  [the longest x1 77.2 us: sample(): pl.pallas_call(functools.partial(sample_kernel, lay), grid_spec=pltpu.Pre...]
    all_to_all x8 -> x0, waiting for transfers between devices: 103 us -> none  [the longest x1 37.1 us: inverse_transform(): lax.all_to_all(first_part, 'row', split_axis=1, concat_axis=2, tiled=True)]
    dot_general x24 -> x0, matrix products: 94.4 us -> none  [contract(): jnp.einsum(form, left, right, precision=PRECISION, preferred_element_type...]
    unnamed x38 -> x22, local copies, waits for them, and re-layouts: 92 us -> 11.4 us
    all_to_all x6 -> x0, other arithmetic: 45.9 us -> none  [the longest x2 16 us: across_columns(): lax.all_to_all(halves[1], 'col', split_axis=2, concat_axis=2, tiled=True)]
    all_to_all x8 -> x0, starting transfers between devices: 39.3 us -> none  [the longest x2 9.83 us: across_columns(): lax.all_to_all(halves[0], 'col', split_axis=2, concat_axis=2, tiled=True)]
    all_to_all x6 -> x0, local copies, waits for them, and re-layouts: 23.5 us -> none  [the longest x1 6.68 us: inverse_transform(): lax.all_to_all(first_part, 'row', split_axis=1, concat_axis=2, tiled=True)]
  transfers between devices with their start and end apart: 12 -> 5, of which waited for: 9 -> 2; matrix products, arithmetic and copies ran while one was open for 31% -> 6% of each run, Pallas kernels for 0% -> 29%
where the time goes in v1:
time: 379 us
  Pallas kernels  281 us (74%)
  waiting for transfers between devices  41.1 us (11%)
  other arithmetic  22.3 us (6%)
  local copies, waits for them, and re-layouts  18 us (5%)
  starting transfers between devices  16.3 us (4%)
    pallas_call x1, Pallas kernels, sample(): pl.pallas_call(functools.partial(sample_kernel, lay), grid_spec=pltpu.Pre...  77.2 us
    pallas_call x1, Pallas kernels, transform(): pl.pallas_call(functools.partial(transform_kernel, lay), in_specs=[vmem]...  66.8 us
    pallas_call x1, Pallas kernels, spread(): pl.pallas_call(functools.partial(spread_kernel, lay), grid_spec=pltpu.Pre...  64.7 us
    ppermute x4, waiting for transfers between devices, share_green(): messages.append(lax.ppermute(sent, ('row', 'col'), pairs))  41.1 us
    pallas_call x1, Pallas kernels, gather_atoms(): pl.pallas_call(functools.partial(gather_kernel, lay), in_specs=[pl.BlockS...  27.5 us
    pallas_call x1, Pallas kernels, return_forces(): pl.pallas_call(functools.partial(return_kernel, lay), in_specs=[pl.BlockS...  21.7 us
    pallas_call x1, Pallas kernels, sort_atoms(): pl.pallas_call(sort_kernel, grid=(frames,), in_specs=[pl.BlockSpec((1, 1,...  18.2 us
    ppermute x4, starting transfers between devices, share_green(): messages.append(lax.ppermute(sent, ('row', 'col'), pairs))  15 us
  transfers between devices with their start and end apart: 5, of which 2 were waited for; matrix products, arithmetic and copies ran while one was open for 6% of the time, Pallas kernels for 29%

profile of v1, /device:TPU:0, one launch (start us, length us, event | category | flops | bytes accessed | tf_op | source)
XLA Modules:
  0.0 379.2 jit_solution(4145677804691378878)
XLA Ops:
  1.1 1.3 collective-permute-start
  7.9 1.1 fusion.17
  10.2 1.6 dynamic-slice_bitcast_fusion
  13.4 1.4 fusion.4
  15.5 18.2 %sort_atoms.1 = (f32[2,8,2048]{2,1,0:T(8,128)S(1)}, f32[2,1,2048]{2,1,0:T(1,128)S(1)}) custom-call(f32[2,1,2048]{2,1,0:T(1,128)S(1)} %get-tuple-element.54.key_row_ref, f32[2,2048,128]{2,1,0:T(8,128)S(1)} %broadcast_in_dim.140.key_col_ref, f32[2,8,2048]{2,1,0:T(8,128)S(1)} %pad_maximum_fusion.3.payload_ref), custom_call_target="tpu_custom_call" | custom-call | tf_op jit(solution)/shard_map/sort_atoms/pallas_call | solution.py:124
  34.4 27.5 %gather_atoms.1.atoms_ref = f32[4,4,8,2048]{3,2,1,0:T(8,128)} custom-call(f32[2,8,2048]{2,1,0:T(8,128)} %copy-done.2), custom_call_target="tpu_custom_call" | custom-call | tf_op jit(solution)/shard_map/gather_atoms/pallas_call | solution.py:303
  61.9 1.9 compare_select_fusion
  64.2 2.3 fusion.1
  66.7 64.7 %spread.1.mesh_ref = f32[4,4608,128]{2,1,0:T(8,128)S(1)} custom-call(s32[256]{0:T(256)S(1)} %get-tuple-element.69.starts_ref, s32[256]{0:T(256)S(1)} %get-tuple-element.68.turns_ref, f32[4,4,8,2048]{3,2,1,0:T(8,128)S(1)} %copy-done, s32[2,32,128]{2,1,0:T(8,128)S(1)} %broadcast_in_dim.149.waves_ref, f32[6,32,128]{2,1,0:T(8,128)S(1)} %broadcast_in_dim.153.cos_ref, ...), custom_call_target="tpu_custom_call" | custom-call | flops 10000000000 | bytes 10000000 | tf_op jit(solution)/shard_map/spread/pallas_call | solution.py:473
  131.5 3.7 copy-done.3
  137.8 1.5 dynamic-slice_bitcast_fusion.4
  139.3 1.7 collective-permute-start.1
  141.0 7.7 %collective-permute-start.4 = (f32[9,64,256]{2,1,0:T(8,128)}, f32[9,64,256]{2,1,0:T(8,128)S(1)}, u32[]{:S(2)}, u32[]{:S(2)}) collective-permute-start(f32[9,64,256]{2,1,0:T(8,128)} %get-tuple-element.42), channel_id=1, source_target_pairs={{0,17},{1,25},{2,19},{3,27},{4,21},{5,29},{6,23},{7,31},{8,1},{9,9... | collective-permute-start | bytes 1769480 | tf_op jit(solution)/shard_map/ppermute | solution.py:850
  148.7 5.5 %collective-permute-start.3 = (f32[9,64,256]{2,1,0:T(8,128)}, f32[9,64,256]{2,1,0:T(8,128)S(1)}, u32[]{:S(2)}, u32[]{:S(2)}) collective-permute-start(f32[9,64,256]{2,1,0:T(8,128)} %get-tuple-element.43), channel_id=1, source_target_pairs={{0,1},{1,9},{2,3},{3,11},{4,5},{5,13},{6,7},{7,15},{8,16},{9,24},{... | collective-permute-start | bytes 1769480 | tf_op jit(solution)/shard_map/ppermute | solution.py:850
  155.9 1.8 fusion
  157.7 17.9 %collective-permute-done.4 = f32[9,64,256]{2,1,0:T(8,128)S(1)} collective-permute-done((f32[9,64,256]{2,1,0:T(8,128)}, f32[9,64,256]{2,1,0:T(8,128)S(1)}, u32[]{:S(2)}, u32[]{:S(2)}) %collective-permute-start.4) | collective-permute-done | bytes 589856 | tf_op jit(solution)/shard_map/ppermute | solution.py:850
  175.6 23.2 %collective-permute-done.3 = f32[9,64,256]{2,1,0:T(8,128)S(1)} collective-permute-done((f32[9,64,256]{2,1,0:T(8,128)}, f32[9,64,256]{2,1,0:T(8,128)S(1)}, u32[]{:S(2)}, u32[]{:S(2)}) %collective-permute-start.3) | collective-permute-done | bytes 589856 | tf_op jit(solution)/shard_map/ppermute | solution.py:850
  198.8 2.7 pad_maximum_fusion.green_ref
  201.5 66.8 %transform.1 = (bf16[4,4608,128]{2,1,0:T(8,128)(2,1)}, bf16[4,4608,128]{2,1,0:T(8,128)(2,1)}) custom-call(f32[4,4608,128]{2,1,0:T(8,128)} %copy-done.3, f32[4,9,64,256]{3,2,1,0:T(8,128)} %pad_maximum_fusion.green_ref, bf16[512,512]{1,0:T(8,128)(2,1)} %get-tuple-element.46.first_high, bf16[512,512]{1,0:T(8,128)(2,1)} %get-tuple-element.45.first_low, ...), custom_call_target="tpu_custom_call" | custom-call | flops 10000000000 | bytes 10000000 | tf_op jit(solution)/shard_map/transform/pallas_call | solution.py:743
  268.2 2.3 copy-done.4
  270.6 2.3 copy-done.5
  272.9 77.2 %sample.1.force_ref = f32[4,4,3,16,128]{4,3,2,1,0:T(8,128)S(1)} custom-call(s32[256]{0:T(256)S(1)} %get-tuple-element.69.starts_ref, s32[256]{0:T(256)S(1)} %get-tuple-element.68.turns_ref, f32[4,4,8,2048]{3,2,1,0:T(8,128)S(1)} %copy-done, s32[2,32,128]{2,1,0:T(8,128)S(1)} %broadcast_in_dim.149.waves_ref, f32[6,32,128]{2,1,0:T(8,128)S(1)} %broadcast_in_dim.153.cos_ref, ...), custom_call_target="tpu_custom_call" | custom-call | flops 10000000000 | bytes 10000000 | tf_op jit(solution)/shard_map/sample/pallas_call | solution.py:537
  350.8 21.7 %return_forces.1 = f32[2,8,3,16,128]{4,3,2,1,0:T(8,128)} custom-call(f32[4,4,3,16,128]{4,3,2,1,0:T(8,128)} %copy-done.1), custom_call_target="tpu_custom_call" | custom-call | tf_op jit(solution)/shard_map/return_forces/pallas_call | solution.py:389
  373.7 4.9 %unsort_forces.1 = f32[2,8,2048]{2,1,0:T(8,128)S(1)} custom-call(f32[2,1,2048]{2,1,0:T(1,128)S(1)} %get-tuple-element.33.rank_ref, f32[2,8,2048]{2,1,0:T(8,128)S(1)} %pad.14.force_ref), custom_call_target="tpu_custom_call" | custom-call | tf_op jit(solution)/shard_map/unsort_forces/pallas_call | solution.py:166
  (71 shorter events, 17.7 us)
Async XLA Ops:
  1.1 135.0 %collective-permute-start = (f32[64,256]{1,0:T(8,128)S(1)}, f32[64,256]{1,0:T(8,128)S(1)}, u32[]{:S(2)}, u32[]{:S(2)}) collective-permute-start(f32[64,256]{1,0:T(8,128)S(1)} %bitcast.63), channel_id=1, source_target_pairs={{4,0},{12,8},{20,16},{28,24}} | collective-permute-start | bytes 196616 | tf_op jit(solution)/shard_map/ppermute | solution.py:826
  12.4 1.0 copy-start.6
  33.7 0.7 copy-start.2
  61.9 4.8 %copy-start = (f32[4,4,8,2048]{3,2,1,0:T(8,128)S(1)}, f32[4,4,8,2048]{3,2,1,0:T(8,128)}, u32[]{:S(2)}) copy-start(f32[4,4,8,2048]{3,2,1,0:T(8,128)} %gather_atoms.1.atoms_ref) | copy-start | bytes 3145732
  66.7 68.4 %copy-start.7 = (f32[272,256]{1,0:T(8,128)S(1)}, f32[272,256]{1,0:T(8,128)}, u32[]{:S(2)}) copy-start(f32[272,256]{1,0:T(8,128)} %get-tuple-element.61) | copy-start | bytes 835588
  131.4 3.7 copy-start.3
  137.8 16.5 %copy-start.8 = (f32[256,256]{1,0:T(8,128)S(1)}, f32[256,256]{1,0:T(8,128)}, u32[]{:S(2)}) copy-start(f32[256,256]{1,0:T(8,128)} %get-tuple-element.64) | copy-start | bytes 786436
  137.8 16.5 %copy-start.9 = (f32[256,256]{1,0:T(8,128)S(1)}, f32[256,256]{1,0:T(8,128)}, u32[]{:S(2)}) copy-start(f32[256,256]{1,0:T(8,128)} %get-tuple-element.65) | copy-start | bytes 786436
  139.3 18.4 %collective-permute-start.1 = (f32[9,64,256]{2,1,0:T(8,128)}, f32[9,64,256]{2,1,0:T(8,128)S(1)}, u32[]{:S(2)}, u32[]{:S(2)}) collective-permute-start(f32[9,64,256]{2,1,0:T(8,128)} %get-tuple-element.41), channel_id=1, source_target_pairs={{0,0},{1,8},{2,2},{3,10},{4,4},{5,12},{6,6},{7,14},{8,17},{9,25},{... | collective-permute-start | bytes 1769480 | tf_op jit(solution)/shard_map/ppermute | solution.py:850
  141.0 34.6 %collective-permute-start.4 = (f32[9,64,256]{2,1,0:T(8,128)}, f32[9,64,256]{2,1,0:T(8,128)S(1)}, u32[]{:S(2)}, u32[]{:S(2)}) collective-permute-start(f32[9,64,256]{2,1,0:T(8,128)} %get-tuple-element.42), channel_id=1, source_target_pairs={{0,17},{1,25},{2,19},{3,27},{4,21},{5,29},{6,23},{7,31},{8,1},{9,9... | collective-permute-start | bytes 1769480 | tf_op jit(solution)/shard_map/ppermute | solution.py:850
  148.7 50.1 %collective-permute-start.3 = (f32[9,64,256]{2,1,0:T(8,128)}, f32[9,64,256]{2,1,0:T(8,128)S(1)}, u32[]{:S(2)}, u32[]{:S(2)}) collective-permute-start(f32[9,64,256]{2,1,0:T(8,128)} %get-tuple-element.43), channel_id=1, source_target_pairs={{0,1},{1,9},{2,3},{3,11},{4,5},{5,13},{6,7},{7,15},{8,16},{9,24},{... | collective-permute-start | bytes 1769480 | tf_op jit(solution)/shard_map/ppermute | solution.py:850
  154.2 44.5 %collective-permute-start.2 = (f32[9,64,256]{2,1,0:T(8,128)}, f32[9,64,256]{2,1,0:T(8,128)}, u32[]{:S(2)}, u32[]{:S(2)}) collective-permute-start(f32[9,64,256]{2,1,0:T(8,128)} %get-tuple-element.44), channel_id=1, source_target_pairs={{0,16},{1,24},{2,18},{3,26},{4,20},{5,28},{6,22},{7,30},{8,0},{9,8... | collective-permute-start | bytes 1769480 | tf_op jit(solution)/shard_map/ppermute | solution.py:850
  268.2 2.3 copy-start.4
  270.6 2.3 copy-start.5
  350.1 0.8 copy-start.1

commit v2 on v1

--- a/solution.py
+++ b/solution.py
@@ -8,9 +8,11 @@
 from jax.experimental.pallas import tpu as pltpu
 from jax.sharding import PartitionSpec as P
 
+
 MESH = pl.DeviceIdType.MESH
 LANES = 128
 CHUNK = 9
+PACK = 4
 HALO = 8
 NT = (((1,), (1,)), ((), ()))
 NN = (((1,), (0,)), ((), ()))
@@ -84,11 +86,15 @@
 
 
 def wave_rows(cosine, sine, cos_ref, sin_ref, rows):
-    even = cos_ref[0] * rows[0]
-    odd = sin_ref[0] * rows[0]
+    copies = cosine.shape[1] // LANES
+
+    def wide(ref, offset):
+        return jnp.concatenate([ref[offset]] * copies, axis=1) * rows[offset]
+
+    even, odd = wide(cos_ref, 0), wide(sin_ref, 0)
     for offset in range(1, 6):
-        even += cos_ref[offset] * rows[offset]
-        odd += sin_ref[offset] * rows[offset]
+        even += wide(cos_ref, offset)
+        odd += wide(sin_ref, offset)
     return cosine * even + sine * odd
 
 
@@ -189,11 +195,13 @@
         self.own = self.slots // 2
         self.slots_padded = max(8, self.slots)
         self.wave_rows = 2 * self.slots_padded
+        self.stride = self.wave_rows + 1
         self.lines = self.half_cols * self.block_cols + HALO
         self.lines_padded = -(-(self.lines + CHUNK - 1) // 8) * 8
         self.splits = self.group // 2
         self.blocks = atoms // LANES
         self.span = self.block_rows + HALO
+        self.pack = math.gcd(PACK, self.blocks)
 
 
 def gather_kernel(lay, mine_ref, all_ref, local_sem, send_sem, recv_sem, pass_sem, took_sem):
@@ -298,7 +306,7 @@
 
 
 def gather_atoms(lay, mine):
-    frames, rows, atoms = mine.shape
+    _, rows, atoms = mine.shape
     dma = pltpu.SemaphoreType.DMA
     return pl.pallas_call(
         functools.partial(gather_kernel, lay),
@@ -397,24 +405,40 @@
     )(forces)
 
 
-def atom_block(lay, atoms_ref, waves_ref, block, with_slopes):
-    lanes = pl.ds(pl.multiple_of(block * LANES, LANES), LANES)
+def atom_group(lay, atoms_ref, waves_ref, group, with_slopes):
+    width = lay.pack * LANES
+    lanes = pl.ds(pl.multiple_of(group * width, width), width)
     piece = atoms_ref[0, 0, :, lanes]
     cells = piece[0:3].astype(jnp.int32)
     values, slopes = spline_rows(piece[3:6])
     charge = piece[6:7]
-    spots = lax.broadcasted_iota(jnp.int32, (lay.span, LANES), 0)
+    spots = lax.broadcasted_iota(jnp.int32, (lay.span, width), 0)
     kinds = [values, slopes] if with_slopes else [values]
     wide = dense(cells[0:1] + HALO - spots, [row_of(kind, 0) for kind in kinds])
-    pad = jnp.zeros((LANES - lay.span, LANES), jnp.float32)
+    pad = jnp.zeros((LANES - lay.span, width), jnp.float32)
     wide = [jnp.concatenate([entry, pad], axis=0) for entry in wide]
-    cosine, sine = phases(waves_ref[0] * cells[2:3] + waves_ref[1], lay.length)
+    turned = jnp.concatenate([waves_ref[0]] * lay.pack, axis=1) * cells[2:3]
+    turned += jnp.concatenate([waves_ref[1]] * lay.pack, axis=1)
+    cosine, sine = phases(turned, lay.length)
     return cells, kinds, charge, wide, cosine, sine
 
 
-def line_weights(cells, kinds, start, lay):
-    lines = lax.broadcasted_iota(jnp.int32, (-(-CHUNK // 8) * 8, LANES), 0) + start
+def line_weights(cells, kinds, starts):
+    lines = lax.broadcasted_iota(jnp.int32, (-(-CHUNK // 8) * 8, LANES), 0)
+    lines = jnp.concatenate([lines + start for start in starts], axis=1)
     return dense(cells[1:2] + HALO - lines, [row_of(kind, 1) for kind in kinds])
+
+
+def lanes_of(block):
+    return slice(block * LANES, (block + 1) * LANES)
+
+
+def pick(kinds, block):
+    return [[row[:, lanes_of(block)] for row in kind] for kind in kinds]
+
+
+def rows_at(lay, line):
+    return pl.ds(pl.multiple_of(line * lay.wave_rows, lay.wave_rows), CHUNK * lay.wave_rows)
 
 
 def spread_kernel(lay, starts_ref, turns_ref, atoms_ref, waves_ref, cos_ref, sin_ref, mesh_ref):
@@ -425,37 +449,55 @@
     def clear():
         mesh_ref[...] = jnp.zeros_like(mesh_ref)
 
-    @pl.loop(0, lay.blocks)
-    def add_block(block):
-        turns = turns_ref[pencil * lay.blocks + block]
-
-        @pl.when(turns > 0)
+    @pl.loop(0, lay.blocks // lay.pack)
+    def add_group(group):
+        base = pencil * lay.blocks + group * lay.pack
+
+        @pl.when(turns_ref[base] > 0)
         def live():
-            cells, kinds, charge, wide, cosine, sine = atom_block(
-                lay, atoms_ref, waves_ref, block, False
+            cells, kinds, charge, wide, cosine, sine = atom_group(
+                lay, atoms_ref, waves_ref, group, False
             )
             waves = wave_rows(cosine, sine, cos_ref, sin_ref, row_of(kinds[0], 2)) * charge
-            high, low = halves_of(wide[0])
-            right = jnp.concatenate(
-                [
-                    jnp.concatenate([high, high], axis=1),
-                    jnp.concatenate([low, low], axis=1),
-                ],
-                axis=0,
-            )
-            start = starts_ref[pencil * lay.blocks + block]
-
-            @pl.loop(0, turns)
-            def add_lines(turn):
-                line = start + turn * CHUNK
-                (weights,) = line_weights(cells, kinds, line, lay)
-                product = jnp.concatenate(
-                    [weights[i : i + 1] * waves for i in range(CHUNK)], axis=0
+            starts = [starts_ref[base + block] for block in range(lay.pack)]
+            (weights,) = line_weights(cells, kinds, starts)
+            rights = []
+            for block in range(lay.pack):
+                high, low = halves_of(wide[0][:, lanes_of(block)])
+                rights.append(
+                    jnp.concatenate(
+                        [
+                            jnp.concatenate([high, high], axis=1),
+                            jnp.concatenate([low, low], axis=1),
+                        ],
+                        axis=0,
+                    )
                 )
+
+            def total_of(weights, block):
+                wave = waves[:, lanes_of(block)]
+                product = jnp.concatenate([weights[i : i + 1] * wave for i in range(CHUNK)], axis=0)
                 high, low = halves_of(product)
-                total = dot(jnp.concatenate([high, low], axis=1), right, NT)
-                where = pl.ds(pl.multiple_of(line * lay.wave_rows, lay.wave_rows), CHUNK * lay.wave_rows)
-                mesh_ref[0, where, :] += total[:, :LANES] + total[:, LANES:]
+                total = dot(jnp.concatenate([high, low], axis=1), rights[block], NT)
+                return total[:, :LANES] + total[:, LANES:]
+
+            totals = [total_of(weights[:, lanes_of(block)], block) for block in range(lay.pack)]
+
+            def add(line, total):
+                for i in range(CHUNK):
+                    part = total[i * lay.wave_rows : (i + 1) * lay.wave_rows]
+                    mesh_ref[0, pl.ds((line + i) * lay.stride, lay.wave_rows), :] += part
+
+            for block in range(lay.pack):
+                add(starts[block], totals[block])
+            for block in range(lay.pack):
+
+                @pl.loop(1, turns_ref[base + block])
+                def more(turn):
+                    line = starts[block] + turn * CHUNK
+                    lanes = lanes_of(block)
+                    (weights,) = line_weights(cells[:, lanes], pick(kinds, block), [line])
+                    add(line, total_of(weights, block))
 
 
 def atom_specs(lay):
@@ -469,7 +511,7 @@
 
 
 def spread(lay, starts, turns, atoms, waves, cosines, sines):
-    size = lay.lines_padded * lay.wave_rows
+    size = -(-lay.lines_padded * lay.stride // 8) * 8
     return pl.pallas_call(
         functools.partial(spread_kernel, lay),
         grid_spec=pltpu.PrefetchScalarGridSpec(
@@ -490,44 +532,72 @@
 ):
     pencil = pl.program_id(0) * lay.half_cols + pl.program_id(1)
 
-    @pl.loop(0, lay.blocks)
-    def sample_block(block):
-        turns = turns_ref[pencil * lay.blocks + block]
-        out_ref[0, 0, :, pl.ds(block, 1), :] = jnp.zeros((3, 1, LANES), jnp.float32)
-
-        @pl.when(turns > 0)
+    @pl.loop(0, lay.blocks // lay.pack)
+    def sample_group(group):
+        base = pencil * lay.blocks + group * lay.pack
+        first = group * lay.pack
+
+        @pl.when(turns_ref[base] == 0)
+        def idle():
+            for block in range(lay.pack):
+                out_ref[0, 0, :, pl.ds(first + block, 1), :] = jnp.zeros((3, 1, LANES), jnp.float32)
+
+        @pl.when(turns_ref[base] > 0)
         def live():
-            cells, kinds, charge, wide, cosine, sine = atom_block(
-                lay, atoms_ref, waves_ref, block, True
+            cells, kinds, charge, wide, cosine, sine = atom_group(
+                lay, atoms_ref, waves_ref, group, True
             )
             third = wave_rows(cosine, sine, cos_ref, sin_ref, row_of(kinds[0], 2))
             third_slope = wave_rows(cosine, sine, cos_ref, sin_ref, row_of(kinds[1], 2))
-            both = jnp.concatenate(wide, axis=1)
-            high, low = halves_of(both)
-            right = jnp.concatenate([high, high], axis=0)
-            start = starts_ref[pencil * lay.blocks + block]
-
-            def add_lines(turn, sums):
-                line = start + turn * CHUNK
-                weights, weight_slopes = line_weights(cells, kinds, line, lay)
-                where = pl.ds(pl.multiple_of(line * lay.wave_rows, lay.wave_rows), CHUNK * lay.wave_rows)
+            starts = [starts_ref[base + block] for block in range(lay.pack)]
+            weights, weight_slopes = line_weights(cells, kinds, starts)
+            rights = []
+            for block in range(lay.pack):
+                both = jnp.concatenate([entry[:, lanes_of(block)] for entry in wide], axis=1)
+                high, low = halves_of(both)
+                rights.append((jnp.concatenate([high, high], axis=0), low))
+
+            def found_at(line, block):
+                where = rows_at(lay, line)
                 field_high = high_ref[0, where, :]
                 field = jnp.concatenate([field_high, low_ref[0, where, :]], axis=1)
-                found = dot(field, right) + dot(field_high, low)
-                plain, sloped, across = sums
+                right, low = rights[block]
+                return dot(field, right) + dot(field_high, low)
+
+            def sums_of(found, weights, weight_slopes):
+                plain = sloped = across = jnp.zeros((lay.wave_rows, LANES), jnp.float32)
                 for i in range(CHUNK):
                     lines = slice(i * lay.wave_rows, (i + 1) * lay.wave_rows)
                     value = found[lines, :LANES]
                     plain += value * weights[i : i + 1]
                     across += value * weight_slopes[i : i + 1]
                     sloped += found[lines, LANES:] * weights[i : i + 1]
-                return plain, sloped, across
-
-            nothing = jnp.zeros((lay.wave_rows, LANES), jnp.float32)
-            plain, sloped, across = lax.fori_loop(0, turns, add_lines, (nothing, nothing, nothing))
-            for dimension, value in enumerate((sloped * third, across * third, plain * third_slope)):
-                total = -charge * jnp.sum(value, axis=0, keepdims=True)
-                out_ref[0, 0, dimension, pl.ds(block, 1), :] = total
+                return sloped, across, plain
+
+            founds = [found_at(starts[block], block) for block in range(lay.pack)]
+            for block in range(lay.pack):
+                lanes = lanes_of(block)
+                sums = sums_of(founds[block], weights[:, lanes], weight_slopes[:, lanes])
+                factors = (third[:, lanes], third[:, lanes], third_slope[:, lanes])
+                for dimension in range(3):
+                    total = jnp.sum(sums[dimension] * factors[dimension], axis=0, keepdims=True)
+                    out_ref[0, 0, dimension, pl.ds(first + block, 1), :] = -charge[:, lanes] * total
+            for block in range(lay.pack):
+
+                @pl.loop(1, turns_ref[base + block])
+                def more(turn):
+                    line = starts[block] + turn * CHUNK
+                    lanes = lanes_of(block)
+                    more_weights, more_slopes = line_weights(
+                        cells[:, lanes], pick(kinds, block), [line]
+                    )
+                    sums = sums_of(found_at(line, block), more_weights, more_slopes)
+                    factors = (third[:, lanes], third[:, lanes], third_slope[:, lanes])
+                    for dimension in range(3):
+                        total = jnp.sum(sums[dimension] * factors[dimension], axis=0, keepdims=True)
+                        out_ref[0, 0, dimension, pl.ds(first + block, 1), :] += (
+                            -charge[:, lanes] * total
+                        )
 
 
 def sample(lay, starts, turns, atoms, waves, cosines, sines, high, low):
@@ -552,34 +622,48 @@
 def transform_kernel(
     lay,
     mesh_ref,
-    green_ref,
-    first_high,
-    first_low,
-    second_high,
-    second_low,
-    back_high,
-    back_low,
-    last_high,
-    last_low,
-    out_high,
-    out_low,
-    field_ref,
-    mine_ref,
-    send_ref,
-    recv_ref,
-    home_ref,
-    extra_ref,
-    send_sem,
-    recv_sem,
-    back_sem,
-    home_sem,
+    *refs,
 ):
+    message_refs = refs[: lay.rows]
+    (
+        first_high,
+        first_low,
+        second_high,
+        second_low,
+        back_high,
+        back_low,
+        last_high,
+        last_low,
+        out_high,
+        out_low,
+        field_ref,
+        mine_ref,
+        send_ref,
+        recv_ref,
+        home_ref,
+        extra_ref,
+        green_ref,
+        send_sem,
+        recv_sem,
+        back_sem,
+        home_sem,
+        green_sem,
+    ) = refs[lay.rows :]
     row = lax.axis_index("row")
     col = lax.axis_index("col")
     side = col % 2
     partner = (row, col + 1 - 2 * side)
     lines, length, own, padded = lay.lines, lay.length, lay.own, lay.slots_padded
     inner = lines - HALO
+
+    number = message_number(lay, row, col)
+
+    def green_copy(index):
+        spot = lax.rem(index - number + lay.rows, lay.rows)
+        return pltpu.make_async_copy(message_refs[index], green_ref.at[spot], green_sem.at[index])
+
+    for index in range(lay.rows):
+        green_copy(index).start()
 
     def three(high, low, table_high, table_low):
         return dot(high, table_high) + dot(low, table_high) + dot(high, table_low)
@@ -607,7 +691,7 @@
     def forward(slot):
         rows = [
             jnp.concatenate(
-                [mesh_ref[r, pl.ds(start, lines, stride=lay.wave_rows), :] for r in range(lay.rows)],
+                [mesh_ref[r, pl.ds(start, lines, stride=lay.stride), :] for r in range(lay.rows)],
                 axis=1,
             )
             for start in (slot, padded + slot)
@@ -643,7 +727,8 @@
     def sent(i):
         push(i).wait_send()
 
-    number = message_number(lay, row, col)
+    for index in range(lay.rows):
+        green_copy(index).wait()
 
     def spectrum(index):
         mine, other = mine_ref[index], recv_ref[index]
@@ -668,7 +753,7 @@
         cos_part, sin_part = found[:length], found[length:]
         real = cos_part[:, :length] + sin_part[:, length:]
         imag = cos_part[:, length:] - sin_part[:, :length]
-        blocks = [green_ref[lax.rem(r + number, lay.rows), index] for r in range(lay.rows)]
+        blocks = [green_ref[r, index] for r in range(lay.rows)]
         green = jnp.concatenate(blocks, axis=0)
         return real * green, imag * green
 
@@ -693,8 +778,8 @@
         send_ref[i, 1] = imag[lines:]
         push_back(i).start()
 
-    cleared = 0 if lay.slots < padded else lines * lay.wave_rows
-    total_rows = lay.lines_padded * lay.wave_rows
+    cleared = 0 if lay.slots < padded else lines * lay.stride // 8 * 8
+    total_rows = mesh_ref.shape[1]
     for r in range(lay.rows):
         field_ref[r, pl.ds(cleared, total_rows - cleared), :] = jnp.zeros(
             (total_rows - cleared, LANES), jnp.float32
@@ -706,7 +791,7 @@
         for part in range(2):
             for r in range(lay.rows):
                 lanes = (part * lay.rows + r) * LANES
-                where = pl.ds(part * padded + local, lines, stride=lay.wave_rows)
+                where = pl.ds(part * padded + local, lines, stride=lay.stride)
                 field_ref[r, where, :] = found[:, lanes : lanes + LANES]
 
     @pl.loop(0, own)
@@ -722,7 +807,8 @@
     def split(line):
         where = pl.ds(pl.multiple_of(line * lay.wave_rows, lay.wave_rows), lay.wave_rows)
         for r in range(lay.rows):
-            out_high[r, where, :], out_low[r, where, :] = halves_of(field_ref[r, where, :])
+            value = field_ref[r, pl.ds(line * lay.stride, lay.wave_rows), :]
+            out_high[r, where, :], out_low[r, where, :] = halves_of(value)
 
     @pl.loop(0, own)
     def returned(i):
@@ -735,14 +821,16 @@
     return (lax.rem(col, 2) * lay.frames + frame) * lay.splits + lax.rem(member, lay.splits)
 
 
-def transform(lay, mesh, green, tables):
+def transform(lay, mesh, messages, tables):
     dma = pltpu.SemaphoreType.DMA
     plane = (2, lay.lines, lay.length)
     vmem = pl.BlockSpec(memory_space=pltpu.VMEM)
-    out = jax.ShapeDtypeStruct(mesh.shape, jnp.bfloat16)
+    out = jax.ShapeDtypeStruct(
+        (lay.rows, lay.lines_padded * lay.wave_rows, LANES), jnp.bfloat16
+    )
     return pl.pallas_call(
         functools.partial(transform_kernel, lay),
-        in_specs=[vmem] * (2 + len(tables)),
+        in_specs=[vmem] + [pl.BlockSpec(memory_space=pl.ANY)] * lay.rows + [vmem] * len(tables),
         out_specs=[vmem, vmem],
         out_shape=[out, out],
         scratch_shapes=[
@@ -752,17 +840,19 @@
             pltpu.VMEM((lay.own + 1,) + plane, jnp.float32),
             pltpu.VMEM((lay.own,) + plane, jnp.float32),
             pltpu.VMEM((2, lay.length, lay.length), jnp.float32),
+            pltpu.VMEM((lay.rows,) + messages[0].shape, jnp.float32),
             dma((lay.own + 1,)),
             dma((lay.own + 1,)),
             dma((lay.own,)),
             dma((lay.own,)),
+            dma((lay.rows,)),
         ],
         compiler_params=pltpu.CompilerParams(
             has_side_effects=True, vmem_limit_bytes=62 * 1024 * 1024
         ),
         cost_estimate=pl.CostEstimate(flops=10**10, bytes_accessed=10**7, transcendentals=0),
         name="transform",
-    )(mesh, green, *tables)
+    )(mesh, *messages, *tables)
 
 
 def table_halves(value):
@@ -848,16 +938,16 @@
                 to_row = to_frame * lay.group + (c % 2) * lay.splits + to_split
                 pairs.append((r * cols + c, to_row * cols + 2 * (c // 2) + to_side))
         messages.append(lax.ppermute(sent, ("row", "col"), pairs))
-    return jnp.stack(messages)
-
-
-def shards(cell_index, fraction, charge, atom_count, influence):
-    frames, unused, atoms = fraction.shape
+    return messages
+
+
+def forces_of(cell_index, fraction, charge, atom_count, influence):
+    frames, _, atoms = fraction.shape
     lay = Layout(frames, influence.shape[2], atoms)
     row = lax.axis_index("row")
     col = lax.axis_index("col")
     side = col % 2
-    green = share_green(lay, influence, row, col)
+    messages = share_green(lay, influence, row, col)
     tables = make_tables(lay, side)
     waves, cosines, sines = make_waves(lay, row, col, side)
 
@@ -884,11 +974,12 @@
     lives = shared[:, :, 7, :].reshape(lines.shape) > 0.5
     lowest = jnp.min(jnp.where(lives, lines, 1024.0), axis=1).astype(jnp.int32)
     highest = jnp.max(jnp.where(lives, lines, -1024.0), axis=1).astype(jnp.int32)
-    starts = lowest + HALO - 5
-    turns = jnp.where(highest >= lowest, (highest - lowest + 6 + CHUNK - 1) // CHUNK, 0)
+    live = highest >= lowest
+    starts = jnp.where(live, lowest + HALO - 5, 0)
+    turns = jnp.where(live, (highest - lowest + 6 + CHUNK - 1) // CHUNK, 0)
 
     mesh = spread(lay, starts, turns, shared, waves, cosines, sines)
-    high, low = transform(lay, mesh, green, tables)
+    high, low = transform(lay, mesh, messages, tables)
     partial = sample(lay, starts, turns, shared, waves, cosines, sines, high, low)
     returned = return_forces(lay, partial)
     forces = jnp.sum(returned, axis=1).reshape(frames, 3, atoms)
@@ -905,5 +996,5 @@
         P("row", "col", None),
     )
     return jax.shard_map(
-        shards, mesh=mesh, in_specs=placed, out_specs=P(None, None, ("row", "col")), check_vma=False
+        forces_of, mesh=mesh, in_specs=placed, out_specs=P(None, None, ("row", "col")), check_vma=False
     )

time: 379 us -> 305 us (0.80)
  Pallas kernels: 281 us -> 221 us
  waiting for transfers between devices: 41.1 us -> 33.1 us
  starting transfers between devices: 16.3 us -> 10.1 us
    pallas_call x1, Pallas kernels: 77.2 us -> 50.8 us  [sample(): pl.pallas_call(functools.partial(sample_kernel, lay), grid_spec=pltpu.Pre...]
    pallas_call x1, Pallas kernels: 64.7 us -> 42.7 us  [spread(): pl.pallas_call(functools.partial(spread_kernel, lay), grid_spec=pltpu.Pre...]
    ppermute x4, waiting for transfers between devices: 41.1 us -> 33.1 us  [share_green(): messages.append(lax.ppermute(sent, ('row', 'col'), pairs))]
    ppermute x4, starting transfers between devices: 15 us -> 8.79 us  [share_green(): messages.append(lax.ppermute(sent, ('row', 'col'), pairs))]
    pallas_call x1, Pallas kernels: 66.8 us -> 60.9 us  [transform(): pl.pallas_call(functools.partial(transform_kernel, lay), in_specs=[vmem]...]
    pallas_call x1, Pallas kernels: 21.7 us -> 16.2 us  [return_forces(): pl.pallas_call(functools.partial(return_kernel, lay), in_specs=[pl.BlockS...]
    unnamed x22 -> x26, local copies, waits for them, and re-layouts: 11.4 us -> 12.2 us
  transfers between devices with their start and end apart: 5 -> 5, of which waited for: 2 -> 2; matrix products, arithmetic and copies ran while one was open for 6% -> 7% of each run, Pallas kernels for 29% -> 29%
where the time goes in v2:
time: 305 us; the launch traced here: 303 us
  Pallas kernels  221 us (72%)
  waiting for transfers between devices  33.1 us (11%)
  other arithmetic  19.6 us (6%)
  local copies, waits for them, and re-layouts  18.6 us (6%)
  starting transfers between devices  10.1 us (3%)
    pallas_call x1, Pallas kernels, transform(): pl.pallas_call(functools.partial(transform_kernel, lay), in_specs=[vmem]...  60.9 us
    pallas_call x1, Pallas kernels, sample(): pl.pallas_call(functools.partial(sample_kernel, lay), grid_spec=pltpu.Pre...  50.8 us
    pallas_call x1, Pallas kernels, spread(): pl.pallas_call(functools.partial(spread_kernel, lay), grid_spec=pltpu.Pre...  42.7 us
    ppermute x4, waiting for transfers between devices, share_green(): messages.append(lax.ppermute(sent, ('row', 'col'), pairs))  33.1 us
    pallas_call x1, Pallas kernels, gather_atoms(): pl.pallas_call(functools.partial(gather_kernel, lay), in_specs=[pl.BlockS...  27.6 us
    pallas_call x1, Pallas kernels, sort_atoms(): pl.pallas_call(sort_kernel, grid=(frames,), in_specs=[pl.BlockSpec((1, 1,...  18.2 us
    pallas_call x1, Pallas kernels, return_forces(): pl.pallas_call(functools.partial(return_kernel, lay), in_specs=[pl.BlockS...  16.2 us
    unnamed x26, local copies, waits for them, and re-layouts  12.2 us
  transfers between devices with their start and end apart: 5, of which 2 were waited for; matrix products, arithmetic and copies ran while one was open for 7% of the time, Pallas kernels for 29%

profile of v2, /device:TPU:0, one launch (start us, length us, event | category | flops | bytes accessed | tf_op | source)
XLA Modules:
  0.0 303.1 jit_solution(10578636057214170416)
XLA Ops:
  1.1 1.3 collective-permute-start
  7.9 1.1 fusion.17
  9.1 1.1 fusion.13
  10.2 1.6 dynamic-slice_bitcast_fusion
  13.4 1.5 fusion.4
  15.6 18.2 %sort_atoms.1 = (f32[2,8,2048]{2,1,0:T(8,128)S(1)}, f32[2,1,2048]{2,1,0:T(1,128)S(1)}) custom-call(f32[2,1,2048]{2,1,0:T(1,128)S(1)} %get-tuple-element.54.key_row_ref, f32[2,2048,128]{2,1,0:T(8,128)S(1)} %broadcast_in_dim.143.key_col_ref, f32[2,8,2048]{2,1,0:T(8,128)S(1)} %pad_maximum_fusion.2.payload_ref), custom_call_target="tpu_custom_call" | custom-call | tf_op jit(solution)/shard_map/sort_atoms/pallas_call | solution.py:130
  34.4 27.6 %gather_atoms.1.atoms_ref = f32[4,4,8,2048]{3,2,1,0:T(8,128)} custom-call(f32[2,8,2048]{2,1,0:T(8,128)} %copy-done.2), custom_call_target="tpu_custom_call" | custom-call | tf_op jit(solution)/shard_map/gather_atoms/pallas_call | solution.py:311
  61.9 2.0 compare_select_fusion.1
  64.2 2.2 fusion.1
  66.7 42.7 %spread.1.mesh_ref = f32[4,4752,128]{2,1,0:T(8,128)S(1)} custom-call(s32[256]{0:T(256)S(1)} %get-tuple-element.65.starts_ref, s32[256]{0:T(256)S(1)} %get-tuple-element.64.turns_ref, f32[4,4,8,2048]{3,2,1,0:T(8,128)S(1)} %copy-done, s32[2,32,128]{2,1,0:T(8,128)S(1)} %broadcast_in_dim.153.waves_ref, f32[6,32,128]{2,1,0:T(8,128)S(1)} %broadcast_in_dim.157.cos_ref, ...), custom_call_target="tpu_custom_call" | custom-call | flops 10000000000 | bytes 10000000 | tf_op jit(solution)/shard_map/spread/pallas_call | solution.py:515
  109.4 3.7 %copy-done.3 = f32[4,4752,128]{2,1,0:T(8,128)} copy-done((f32[4,4752,128]{2,1,0:T(8,128)}, f32[4,4752,128]{2,1,0:T(8,128)S(1)}, u32[]{:S(2)}) %copy-start.3) | copy-done | bytes 9732120
  115.8 1.3 dynamic-slice_bitcast_fusion.1
  117.1 2.4 collective-permute-start.4
  119.5 3.8 %collective-permute-start.3 = (f32[9,64,256]{2,1,0:T(8,128)}, f32[9,64,256]{2,1,0:T(8,128)S(1)}, u32[]{:S(2)}, u32[]{:S(2)}) collective-permute-start(f32[9,64,256]{2,1,0:T(8,128)} %get-tuple-element.42), channel_id=1, source_target_pairs={{0,1},{1,9},{2,3},{3,11},{4,5},{5,13},{6,7},{7,15},{8,16},{9,24},{... | collective-permute-start | bytes 1769480 | tf_op jit(solution)/shard_map/ppermute | solution.py:940
  124.4 1.5 collective-permute-start.1
  127.5 1.8 fusion
  129.3 8.0 %collective-permute-done.4.refs_3_ = f32[9,64,256]{2,1,0:T(8,128)S(1)} collective-permute-done((f32[9,64,256]{2,1,0:T(8,128)}, f32[9,64,256]{2,1,0:T(8,128)S(1)}, u32[]{:S(2)}, u32[]{:S(2)}) %collective-permute-start.4) | collective-permute-done | bytes 589856 | tf_op jit(solution)/shard_map/ppermute | solution.py:940
  137.3 25.0 %collective-permute-done.3.refs_2_ = f32[9,64,256]{2,1,0:T(8,128)S(1)} collective-permute-done((f32[9,64,256]{2,1,0:T(8,128)}, f32[9,64,256]{2,1,0:T(8,128)S(1)}, u32[]{:S(2)}, u32[]{:S(2)}) %collective-permute-start.3) | collective-permute-done | bytes 589856 | tf_op jit(solution)/shard_map/ppermute | solution.py:940
  163.1 60.9 %transform.1 = (bf16[4,4608,128]{2,1,0:T(8,128)(2,1)}, bf16[4,4608,128]{2,1,0:T(8,128)(2,1)}) custom-call(f32[4,4752,128]{2,1,0:T(8,128)} %copy-done.3, f32[9,64,256]{2,1,0:T(8,128)} %collective-permute-done.1.refs_0_, f32[9,64,256]{2,1,0:T(8,128)} %collective-permute-done.2.refs_1_, f32[9,64,256]{2,1,0:T(8,128)} %copy-done.11, f32[9,64,256]{2,1,0:T(8,128)} %copy-done.10, ...), custom_call_target="tpu_custom_call" | custom-call | flops 10000000000 | bytes 10000000 | tf_op jit(solution)/shard_map/transform/pallas_call | solution.py:831
  224.1 2.3 copy-done.4
  226.4 2.3 copy-done.5
  228.7 50.8 %sample.1.force_ref = f32[4,4,3,16,128]{4,3,2,1,0:T(8,128)S(1)} custom-call(s32[256]{0:T(256)S(1)} %get-tuple-element.65.starts_ref, s32[256]{0:T(256)S(1)} %get-tuple-element.64.turns_ref, f32[4,4,8,2048]{3,2,1,0:T(8,128)S(1)} %copy-done, s32[2,32,128]{2,1,0:T(8,128)S(1)} %broadcast_in_dim.153.waves_ref, f32[6,32,128]{2,1,0:T(8,128)S(1)} %broadcast_in_dim.157.cos_ref, ...), custom_call_target="tpu_custom_call" | custom-call | flops 10000000000 | bytes 10000000 | tf_op jit(solution)/shard_map/sample/pallas_call | solution.py:607
  280.3 16.2 %return_forces.1 = f32[2,8,3,16,128]{4,3,2,1,0:T(8,128)} custom-call(f32[4,4,3,16,128]{4,3,2,1,0:T(8,128)} %copy-done.1), custom_call_target="tpu_custom_call" | custom-call | tf_op jit(solution)/shard_map/return_forces/pallas_call | solution.py:397
  297.5 4.9 %unsort_forces.1 = f32[2,8,2048]{2,1,0:T(8,128)S(1)} custom-call(f32[2,1,2048]{2,1,0:T(1,128)S(1)} %get-tuple-element.33.rank_ref, f32[2,8,2048]{2,1,0:T(8,128)S(1)} %pad.14.force_ref), custom_call_target="tpu_custom_call" | custom-call | tf_op jit(solution)/shard_map/unsort_forces/pallas_call | solution.py:172
  (74 shorter events, 18.4 us)
Async XLA Ops:
  1.1 113.0 %collective-permute-start = (f32[64,256]{1,0:T(8,128)S(1)}, f32[64,256]{1,0:T(8,128)S(1)}, u32[]{:S(2)}, u32[]{:S(2)}) collective-permute-start(f32[64,256]{1,0:T(8,128)S(1)} %bitcast.56), channel_id=1, source_target_pairs={{4,0},{12,8},{20,16},{28,24}} | collective-permute-start | bytes 196616 | tf_op jit(solution)/shard_map/ppermute | solution.py:916
  12.4 1.0 copy-start.6
  33.7 0.6 copy-start.2
  61.9 4.8 %copy-start = (f32[4,4,8,2048]{3,2,1,0:T(8,128)S(1)}, f32[4,4,8,2048]{3,2,1,0:T(8,128)}, u32[]{:S(2)}) copy-start(f32[4,4,8,2048]{3,2,1,0:T(8,128)} %gather_atoms.1.atoms_ref) | copy-start | bytes 3145732
  66.7 46.4 %copy-start.7 = (f32[272,256]{1,0:T(8,128)S(1)}, f32[272,256]{1,0:T(8,128)}, u32[]{:S(2)}) copy-start(f32[272,256]{1,0:T(8,128)} %get-tuple-element.61) | copy-start | bytes 835588
  109.4 3.7 %copy-start.3 = (f32[4,4752,128]{2,1,0:T(8,128)}, f32[4,4752,128]{2,1,0:T(8,128)S(1)}, u32[]{:S(2)}) copy-start(f32[4,4752,128]{2,1,0:T(8,128)S(1)} %spread.1.mesh_ref) | copy-start | bytes 29196292
  115.8 10.1 %copy-start.8 = (f32[256,256]{1,0:T(8,128)S(1)}, f32[256,256]{1,0:T(8,128)}, u32[]{:S(2)}) copy-start(f32[256,256]{1,0:T(8,128)} %get-tuple-element.66) | copy-start | bytes 786436
  115.8 10.1 %copy-start.9 = (f32[256,256]{1,0:T(8,128)S(1)}, f32[256,256]{1,0:T(8,128)}, u32[]{:S(2)}) copy-start(f32[256,256]{1,0:T(8,128)} %get-tuple-element.67) | copy-start | bytes 786436
  117.1 20.2 %collective-permute-start.4 = (f32[9,64,256]{2,1,0:T(8,128)}, f32[9,64,256]{2,1,0:T(8,128)S(1)}, u32[]{:S(2)}, u32[]{:S(2)}) collective-permute-start(f32[9,64,256]{2,1,0:T(8,128)} %get-tuple-element.41), channel_id=1, source_target_pairs={{0,17},{1,25},{2,19},{3,27},{4,21},{5,29},{6,23},{7,31},{8,1},{9,9... | collective-permute-start | bytes 1769480 | tf_op jit(solution)/shard_map/ppermute | solution.py:940
  119.5 42.8 %collective-permute-start.3 = (f32[9,64,256]{2,1,0:T(8,128)}, f32[9,64,256]{2,1,0:T(8,128)S(1)}, u32[]{:S(2)}, u32[]{:S(2)}) collective-permute-start(f32[9,64,256]{2,1,0:T(8,128)} %get-tuple-element.42), channel_id=1, source_target_pairs={{0,1},{1,9},{2,3},{3,11},{4,5},{5,13},{6,7},{7,15},{8,16},{9,24},{... | collective-permute-start | bytes 1769480 | tf_op jit(solution)/shard_map/ppermute | solution.py:940
  123.3 39.0 %collective-permute-start.2 = (f32[9,64,256]{2,1,0:T(8,128)}, f32[9,64,256]{2,1,0:T(8,128)}, u32[]{:S(2)}, u32[]{:S(2)}) collective-permute-start(f32[9,64,256]{2,1,0:T(8,128)} %get-tuple-element.43), channel_id=1, source_target_pairs={{0,16},{1,24},{2,18},{3,26},{4,20},{5,28},{6,22},{7,30},{8,0},{9,8... | collective-permute-start | bytes 1769480 | tf_op jit(solution)/shard_map/ppermute | solution.py:940
  124.4 37.9 %collective-permute-start.1 = (f32[9,64,256]{2,1,0:T(8,128)S(1)}, f32[9,64,256]{2,1,0:T(8,128)}, u32[]{:S(2)}, u32[]{:S(2)}) collective-permute-start(f32[9,64,256]{2,1,0:T(8,128)S(1)} %get-tuple-element.44), channel_id=1, source_target_pairs={{0,0},{1,8},{2,2},{3,10},{4,4},{5,12},{6,6},{7,14},{8,17},{9,25},{... | collective-permute-start | bytes 1769480 | tf_op jit(solution)/shard_map/ppermute | solution.py:940
  137.3 25.1 %copy-start.10 = (f32[9,64,256]{2,1,0:T(8,128)}, f32[9,64,256]{2,1,0:T(8,128)S(1)}, u32[]{:S(2)}) copy-start(f32[9,64,256]{2,1,0:T(8,128)S(1)} %collective-permute-done.4.refs_3_) | copy-start | bytes 1769476
  162.3 0.8 copy-start.11
  224.1 2.3 copy-start.4
  226.4 2.3 copy-start.5
  279.6 0.7 copy-start.1

commit v3 on v2

--- a/solution.py
+++ b/solution.py
@@ -3,6 +3,7 @@
 
 import jax
 import jax.numpy as jnp
+import numpy as np
 from jax import lax
 from jax.experimental import pallas as pl
 from jax.experimental.pallas import tpu as pltpu
@@ -11,7 +12,7 @@
 
 MESH = pl.DeviceIdType.MESH
 LANES = 128
-CHUNK = 9
+CHUNK = 10
 PACK = 4
 HALO = 8
 NT = (((1,), (1,)), ((), ()))
@@ -58,7 +59,11 @@
 
 
 def row_of(lists, dimension):
-    return [entry[dimension : dimension + 1, :] for entry in lists]
+    starts = range(dimension, lists[0].shape[0], 3)
+    return [
+        jnp.concatenate([entry[start : start + 1, :] for start in starts], axis=1)
+        for entry in lists
+    ]
 
 
 def phases(product, length):
@@ -85,7 +90,7 @@
     return cosine, sine
 
 
-def wave_rows(cosine, sine, cos_ref, sin_ref, rows):
+def wave_rows(cosine, sine, cos_ref, sin_ref, packed_ref, cells, rows):
     copies = cosine.shape[1] // LANES
 
     def wide(ref, offset):
@@ -95,17 +100,43 @@
     for offset in range(1, 6):
         even += wide(cos_ref, offset)
         odd += wide(sin_ref, offset)
-    return cosine * even + sine * odd
-
-
-def sort_kernel(key_row_ref, key_col_ref, payload_ref, sorted_ref, rank_ref):
-    atoms = key_row_ref.shape[2]
-
-    @pl.loop(0, atoms // LANES)
-    def count(part):
-        lanes = pl.ds(pl.multiple_of(part * LANES, LANES), LANES)
-        below = key_col_ref[0] < key_row_ref[0, :, lanes]
-        rank_ref[0, :, lanes] = jnp.sum(jnp.where(below, 1.0, 0.0), axis=0, keepdims=True)
+    real = cosine * even + sine * odd
+    imag = cosine * odd - sine * even
+    middle = rows[0] - rows[1] + rows[2] - rows[3] + rows[4] - rows[5]
+    middle = jnp.where((cells & 1) == 0, middle, -middle)
+    packed = jnp.concatenate([packed_ref[...]] * copies, axis=1)
+    return jnp.concatenate([real, jnp.where(packed > 0.5, middle, imag)], axis=0)
+
+
+def sort_kernel(bins, width, payload_ref, sorted_ref, rank_ref):
+    atoms = payload_ref.shape[2]
+    blocks = atoms // LANES
+    line = payload_ref[0, 1:2, :]
+    line = line - width * jnp.floor((line + 0.5) * (1.0 / width))
+    line = jnp.where(payload_ref[0, 7:8, :] > 0.5, line.astype(jnp.int32), bins - 1)
+    kinds = lax.broadcasted_iota(jnp.int32, (bins, LANES), 0)
+    marks = [jnp.where(line[:, lanes_of(block)] == kinds, 1.0, 0.0) for block in range(blocks)]
+    across = lax.broadcasted_iota(jnp.int32, (LANES, LANES), 0)
+    down = lax.broadcasted_iota(jnp.int32, (LANES, LANES), 1)
+    before = jnp.where(across < down, 1.0, 0.0).astype(jnp.bfloat16)
+    every = jnp.ones((LANES, LANES), jnp.bfloat16)
+    packed = jnp.concatenate(marks, axis=0).astype(jnp.bfloat16)
+    earlier = dot(packed, before)
+    counts = dot(packed, every)
+    running = jnp.zeros((bins, LANES), jnp.float32)
+    partial = []
+    for block in range(blocks):
+        partial.append(running + earlier[block * bins : (block + 1) * bins])
+        running += counts[block * bins : (block + 1) * bins]
+    lower = lax.broadcasted_iota(jnp.int32, (bins, bins), 1) < lax.broadcasted_iota(
+        jnp.int32, (bins, bins), 0
+    )
+    lower = jnp.where(lower, 1.0, 0.0).astype(jnp.bfloat16)
+    high, low = halves_of(running)
+    base = dot(lower, high) + dot(lower, low)
+    for block in range(blocks):
+        places = marks[block] * (partial[block] + base)
+        rank_ref[0, :, block * LANES : (block + 1) * LANES] = jnp.sum(places, axis=0, keepdims=True)
 
     value = payload_ref[0]
     first, rest = halves_of(value)
@@ -113,28 +144,25 @@
     third = (left - rest.astype(jnp.float32)).astype(jnp.bfloat16)
     pieces = jnp.concatenate([first, rest, third, jnp.zeros_like(first)], axis=0)
     rank = rank_ref[0].astype(jnp.int32)
-    width = math.gcd(256, atoms)
-
-    @pl.loop(0, atoms // width)
+    size = math.gcd(256, atoms)
+
+    @pl.loop(0, atoms // size)
     def place(part):
-        start = pl.multiple_of(part * width, width)
-        spots = lax.broadcasted_iota(jnp.int32, (width, atoms), 0) + start
+        start = pl.multiple_of(part * size, size)
+        spots = lax.broadcasted_iota(jnp.int32, (size, atoms), 0) + start
         chosen = jnp.where(rank == spots, 1.0, 0.0).astype(jnp.bfloat16)
         moved = dot(pieces, chosen, NT)
-        sorted_ref[0, :, pl.ds(start, width)] = moved[0:8] + moved[8:16] + moved[16:24]
-
-
-def sort_atoms(key_row, key_col, payload):
+        sorted_ref[0, :, pl.ds(start, size)] = moved[0:8] + moved[8:16] + moved[16:24]
+
+
+def sort_atoms(lay, payload):
     frames, rows, atoms = payload.shape
     whole = lambda frame: (frame, 0, 0)
+    bins = -(-(lay.block_cols + 1) // 16) * 16
     return pl.pallas_call(
-        sort_kernel,
+        functools.partial(sort_kernel, bins, lay.block_cols),
         grid=(frames,),
-        in_specs=[
-            pl.BlockSpec((1, 1, atoms), whole),
-            pl.BlockSpec((1, atoms, LANES), whole),
-            pl.BlockSpec((1, rows, atoms), whole),
-        ],
+        in_specs=[pl.BlockSpec((1, rows, atoms), whole)],
         out_specs=[pl.BlockSpec((1, rows, atoms), whole), pl.BlockSpec((1, 1, atoms), whole)],
         out_shape=[
             jax.ShapeDtypeStruct((frames, rows, atoms), jnp.float32),
@@ -142,7 +170,7 @@
         ],
         compiler_params=pltpu.CompilerParams(vmem_limit_bytes=32 * 1024 * 1024),
         name="sort_atoms",
-    )(key_row, key_col, payload)
+    )(payload)
 
 
 def unsort_kernel(rank_ref, force_ref, out_ref):
@@ -214,6 +242,10 @@
     hub = half == side
     pair_start = (2 * pair) % lay.half_cols
 
+    def nearest(step):
+        other = lax.rem(row // lay.group + step // lay.group, lay.frames)
+        return other * lay.group + lax.rem(row + step, lay.group)
+
     def first_send(frame, member):
         target = frame * lay.group + member
         index = frame * lay.group + member
@@ -265,7 +297,8 @@
 
     @pl.when(hub)
     def forward():
-        for source in range(lay.rows):
+        for step in range(lay.rows):
+            source = nearest(step)
             for part in range(2):
                 spot = pair_start + part
                 alone = (source == row) & (part == side)
@@ -410,15 +443,15 @@
     lanes = pl.ds(pl.multiple_of(group * width, width), width)
     piece = atoms_ref[0, 0, :, lanes]
     cells = piece[0:3].astype(jnp.int32)
-    values, slopes = spline_rows(piece[3:6])
+    packed = [piece[3:6, lanes_of(block)] for block in range(lay.pack)]
+    values, slopes = spline_rows(jnp.concatenate(packed, axis=0))
     charge = piece[6:7]
     spots = lax.broadcasted_iota(jnp.int32, (lay.span, width), 0)
     kinds = [values, slopes] if with_slopes else [values]
     wide = dense(cells[0:1] + HALO - spots, [row_of(kind, 0) for kind in kinds])
     pad = jnp.zeros((LANES - lay.span, width), jnp.float32)
     wide = [jnp.concatenate([entry, pad], axis=0) for entry in wide]
-    turned = jnp.concatenate([waves_ref[0]] * lay.pack, axis=1) * cells[2:3]
-    turned += jnp.concatenate([waves_ref[1]] * lay.pack, axis=1)
+    turned = jnp.concatenate([waves_ref[...]] * lay.pack, axis=1) * cells[2:3]
     cosine, sine = phases(turned, lay.length)
     return cells, kinds, charge, wide, cosine, sine
 
@@ -434,14 +467,16 @@
 
 
 def pick(kinds, block):
-    return [[row[:, lanes_of(block)] for row in kind] for kind in kinds]
+    return [[row[3 * block : 3 * block + 3] for row in kind] for kind in kinds]
 
 
 def rows_at(lay, line):
     return pl.ds(pl.multiple_of(line * lay.wave_rows, lay.wave_rows), CHUNK * lay.wave_rows)
 
 
-def spread_kernel(lay, starts_ref, turns_ref, atoms_ref, waves_ref, cos_ref, sin_ref, mesh_ref):
+def spread_kernel(
+    lay, starts_ref, turns_ref, atoms_ref, waves_ref, packed_ref, cos_ref, sin_ref, mesh_ref
+):
     part = pl.program_id(1)
     pencil = pl.program_id(0) * lay.half_cols + part
 
@@ -458,7 +493,8 @@
             cells, kinds, charge, wide, cosine, sine = atom_group(
                 lay, atoms_ref, waves_ref, group, False
             )
-            waves = wave_rows(cosine, sine, cos_ref, sin_ref, row_of(kinds[0], 2)) * charge
+            tables = cosine, sine, cos_ref, sin_ref, packed_ref
+            waves = wave_rows(*tables, cells[2:3], row_of(kinds[0], 2)) * charge
             starts = [starts_ref[base + block] for block in range(lay.pack)]
             (weights,) = line_weights(cells, kinds, starts)
             rights = []
@@ -504,13 +540,14 @@
     fixed = lambda row, part, *refs: (0, 0, 0)
     return [
         pl.BlockSpec((1, 1, 8, lay.atoms), lambda row, part, *refs: (row, part, 0, 0)),
-        pl.BlockSpec((2, lay.wave_rows, LANES), fixed),
-        pl.BlockSpec((6, lay.wave_rows, LANES), fixed),
-        pl.BlockSpec((6, lay.wave_rows, LANES), fixed),
+        pl.BlockSpec((lay.slots_padded, LANES), lambda row, part, *refs: (0, 0)),
+        pl.BlockSpec((lay.slots_padded, LANES), lambda row, part, *refs: (0, 0)),
+        pl.BlockSpec((6, lay.slots_padded, LANES), fixed),
+        pl.BlockSpec((6, lay.slots_padded, LANES), fixed),
     ]
 
 
-def spread(lay, starts, turns, atoms, waves, cosines, sines):
+def spread(lay, starts, turns, atoms, waves):
     size = -(-lay.lines_padded * lay.stride // 8) * 8
     return pl.pallas_call(
         functools.partial(spread_kernel, lay),
@@ -524,11 +561,21 @@
         compiler_params=pltpu.CompilerParams(vmem_limit_bytes=40 * 1024 * 1024),
         cost_estimate=pl.CostEstimate(flops=10**10, bytes_accessed=10**7, transcendentals=0),
         name="spread",
-    )(starts, turns, atoms, waves, cosines, sines)
+    )(starts, turns, atoms, *waves)
 
 
 def sample_kernel(
-    lay, starts_ref, turns_ref, atoms_ref, waves_ref, cos_ref, sin_ref, high_ref, low_ref, out_ref
+    lay,
+    starts_ref,
+    turns_ref,
+    atoms_ref,
+    waves_ref,
+    packed_ref,
+    cos_ref,
+    sin_ref,
+    high_ref,
+    low_ref,
+    out_ref,
 ):
     pencil = pl.program_id(0) * lay.half_cols + pl.program_id(1)
 
@@ -547,8 +594,9 @@
             cells, kinds, charge, wide, cosine, sine = atom_group(
                 lay, atoms_ref, waves_ref, group, True
             )
-            third = wave_rows(cosine, sine, cos_ref, sin_ref, row_of(kinds[0], 2))
-            third_slope = wave_rows(cosine, sine, cos_ref, sin_ref, row_of(kinds[1], 2))
+            tables = cosine, sine, cos_ref, sin_ref, packed_ref
+            third = wave_rows(*tables, cells[2:3], row_of(kinds[0], 2))
+            third_slope = wave_rows(*tables, cells[2:3], row_of(kinds[1], 2))
             starts = [starts_ref[base + block] for block in range(lay.pack)]
             weights, weight_slopes = line_weights(cells, kinds, starts)
             rights = []
@@ -600,7 +648,7 @@
                         )
 
 
-def sample(lay, starts, turns, atoms, waves, cosines, sines, high, low):
+def sample(lay, starts, turns, atoms, waves, high, low):
     size = lay.lines_padded * lay.wave_rows
     field = pl.BlockSpec((1, size, LANES), lambda row, part, *refs: (row, 0, 0))
     shape = (lay.rows, lay.half_cols, 3, lay.blocks, LANES)
@@ -616,7 +664,7 @@
         compiler_params=pltpu.CompilerParams(vmem_limit_bytes=40 * 1024 * 1024),
         cost_estimate=pl.CostEstimate(flops=10**10, bytes_accessed=10**7, transcendentals=0),
         name="sample",
-    )(starts, turns, atoms, waves, cosines, sines, high, low)
+    )(starts, turns, atoms, *waves, high, low)
 
 
 def transform_kernel(
@@ -786,13 +834,15 @@
         )
 
     def last(local, planes_ref, i):
-        high, low = halves_of(jnp.concatenate([planes_ref[i, 0], planes_ref[i, 1]], axis=1))
+        high, low = halves_of(jnp.concatenate([planes_ref[i, 0], planes_ref[i, 1]], axis=0))
         found = three(high, low, last_high[...], last_low[...])
-        for part in range(2):
+        width = lay.rows * LANES
+        real = found[:lines, :width] - found[lines:, width:]
+        imag = found[:lines, width:] + found[lines:, :width]
+        for part, value in enumerate((real, imag)):
+            where = pl.ds(part * padded + local, lines, stride=lay.stride)
             for r in range(lay.rows):
-                lanes = (part * lay.rows + r) * LANES
-                where = pl.ds(part * padded + local, lines, stride=lay.stride)
-                field_ref[r, where, :] = found[:, lanes : lanes + LANES]
+                field_ref[r, where, :] = value[:, r * LANES : (r + 1) * LANES]
 
     @pl.loop(0, own)
     def last_mine(i):
@@ -860,29 +910,31 @@
     return leading.astype(jnp.bfloat16), (value - leading).astype(jnp.bfloat16)
 
 
-def make_tables(lay, side):
+def constant_halves(value):
+    high = value.astype(jnp.bfloat16)
+    return high, (value - high.astype(np.float64)).astype(jnp.bfloat16)
+
+
+def make_tables(lay):
     length, half = lay.length, lay.half_cols * lay.block_cols
+    waves = np.arange(length)
+    spots = np.arange(LANES)
+    across = (np.arange(lay.rows)[:, None] * lay.block_rows + spots[None, :] - HALO).reshape(-1)
+    valid = np.tile(spots < lay.span, lay.rows)
+    angle = across[:, None] * waves[None, :] % length * (2.0 * np.pi / length)
+    cosine = np.where(valid[:, None], np.cos(angle), 0.0)
+    sine = np.where(valid[:, None], np.sin(angle), 0.0)
+    first = constant_halves(np.concatenate([cosine, sine], axis=1))
+    last = constant_halves(np.concatenate([cosine.T, sine.T], axis=1))
+    zero = lax.optimization_barrier(jnp.int32(0))
     waves = jnp.arange(length, dtype=jnp.int32)
-    spots = jnp.arange(LANES, dtype=jnp.int32)
-    blocks = jnp.arange(lay.rows, dtype=jnp.int32)
-    zero = lax.optimization_barrier(jnp.int32(0))
-    across = (blocks[:, None] * lay.block_rows + spots[None, :] - HALO).reshape(-1) + length + zero
-    valid = jnp.tile(spots < lay.span, lay.rows)
-    cosine, sine = phases(across[:, None] * waves[None, :], length)
-    keep = valid[:, None]
-    first = jnp.where(keep, jnp.concatenate([cosine, sine], axis=1), 0.0)
-    cosine, sine = phases(across[None, :] * waves[:, None], length)
-    top = jnp.concatenate([cosine, sine], axis=1)
-    bottom = jnp.concatenate([-sine, cosine], axis=1)
-    last = jnp.where(jnp.tile(valid, 2)[None, :], jnp.concatenate([top, bottom], axis=0), 0.0)
-    along = waves + half * side
-    second = jnp.concatenate(phases(waves[:, None] * along[None, :], length), axis=0)
-    near = jnp.arange(lay.lines, dtype=jnp.int32) - HALO + length
-    both = jnp.concatenate([near + half * side, near + half * (1 - side)])
+    second = jnp.concatenate(phases(waves[:, None] * (waves[None, :] + zero), length), axis=0)
+    near = jnp.arange(lay.lines, dtype=jnp.int32) - HALO + length + zero
+    both = jnp.concatenate([near, near + half])
     back = jnp.concatenate(phases(both[:, None] * waves[None, :], length), axis=0)
     tables = []
-    for table in (first, second, back, last):
-        tables.extend(table_halves(table))
+    for pair in (first, table_halves(second), table_halves(back), last):
+        tables.extend(pair)
     return tables
 
 
@@ -894,17 +946,20 @@
     start = lay.block_cols * source + jnp.where(source >= lay.half_cols, 1, 0) + split * lay.slots
     index = jnp.arange(lay.slots_padded, dtype=jnp.int32)
     slot = jnp.where(index < lay.own, (1 - side) * lay.own, side * lay.own) + index % lay.own
-    special = (source == 0) & (split == 0) & (slot == 0)
-    waves = jnp.concatenate([start + slot, jnp.where(special, length // 2, start + slot)])
-    turns = jnp.concatenate([jnp.zeros_like(slot), jnp.where(special, 0, length // 4)])
-    live = jnp.tile(index < lay.slots, 2)[None, :, None]
+    waves = start + slot
+    packed = (source == 0) & (split == 0) & (slot == 0) & (index < lay.slots)
+    live = (index < lay.slots)[None, :, None]
     offsets = jnp.arange(6, dtype=jnp.int32)
     cosine, sine = phases(offsets[:, None] * waves[None, :], length)
-    shape = (6, lay.wave_rows, LANES)
-    cosines = jnp.broadcast_to(jnp.where(live, cosine[:, :, None], 0.0), shape)
-    sines = jnp.broadcast_to(jnp.where(live, sine[:, :, None], 0.0), shape)
-    both = jnp.broadcast_to(jnp.stack([waves, turns])[:, :, None], (2, lay.wave_rows, LANES))
-    return both, cosines, sines
+    shape = (lay.slots_padded, LANES)
+    cosines = jnp.broadcast_to(jnp.where(live, cosine[:, :, None], 0.0), (6,) + shape)
+    sines = jnp.broadcast_to(jnp.where(live, sine[:, :, None], 0.0), (6,) + shape)
+    return (
+        jnp.broadcast_to(waves[:, None], shape),
+        jnp.broadcast_to(packed[:, None].astype(jnp.float32), shape),
+        cosines,
+        sines,
+    )
 
 
 def share_green(lay, influence, row, col):
@@ -948,8 +1003,8 @@
     col = lax.axis_index("col")
     side = col % 2
     messages = share_green(lay, influence, row, col)
-    tables = make_tables(lay, side)
-    waves, cosines, sines = make_waves(lay, row, col, side)
+    tables = make_tables(lay)
+    waves = make_waves(lay, row, col, side)
 
     slot_ids = jnp.arange(atoms, dtype=jnp.int32)
     alive = slot_ids[None, :] < atom_count
@@ -965,9 +1020,7 @@
         ],
         axis=1,
     )
-    key = (jnp.where(alive, cells[:, 1], lay.length) * atoms + slot_ids[None, :]).astype(jnp.float32)
-    key_col = jnp.broadcast_to(key[:, :, None], (frames, atoms, LANES))
-    sorted_atoms, rank = sort_atoms(key[:, None, :], key_col, payload)
+    sorted_atoms, rank = sort_atoms(lay, payload)
     shared = gather_atoms(lay, sorted_atoms)
 
     lines = shared[:, :, 1, :].reshape(lay.rows * lay.half_cols * lay.blocks, LANES)
@@ -978,9 +1031,9 @@
     starts = jnp.where(live, lowest + HALO - 5, 0)
     turns = jnp.where(live, (highest - lowest + 6 + CHUNK - 1) // CHUNK, 0)
 
-    mesh = spread(lay, starts, turns, shared, waves, cosines, sines)
+    mesh = spread(lay, starts, turns, shared, waves)
     high, low = transform(lay, mesh, messages, tables)
-    partial = sample(lay, starts, turns, shared, waves, cosines, sines, high, low)
+    partial = sample(lay, starts, turns, shared, waves, high, low)
     returned = return_forces(lay, partial)
     forces = jnp.sum(returned, axis=1).reshape(frames, 3, atoms)
     forces = jnp.pad(forces, ((0, 0), (0, 5), (0, 0)))

time: 305 us -> 228 us (0.75)
  waiting for transfers between devices: 33.1 us -> 0.01 us
  Pallas kernels: 221 us -> 189 us
  other arithmetic: 19.6 us -> 9.64 us
    ppermute x4, waiting for transfers between devices: 33.1 us -> 0.01 us  [share_green(): messages.append(lax.ppermute(sent, ('row', 'col'), pairs))]
    pallas_call x1, Pallas kernels: 18.2 us -> 7.76 us  [sort_atoms(): pl.pallas_call(functools.partial(sort_kernel, bins, lay.block_cols), grid...]
    pallas_call x1, Pallas kernels: 42.7 us -> 32.3 us  [spread(): pl.pallas_call(functools.partial(spread_kernel, lay), grid_spec=pltpu.Pre...]
    pallas_call x1, Pallas kernels: 50.8 us -> 41 us  [sample(): pl.pallas_call(functools.partial(sample_kernel, lay), grid_spec=pltpu.Pre...]
    convert_element_type x4 -> x2, other arithmetic: 5.88 us -> 1.75 us  [table_halves(): (value - leading).astype(jnp.bfloat16)]
    unnamed x26 -> x28, local copies, waits for them, and re-layouts: 12.2 us -> 12.6 us
  transfers between devices with their start and end apart: 5 -> 5, of which waited for: 2 -> 0; matrix products, arithmetic and copies ran while one was open for 7% -> 5% of each run, Pallas kernels for 29% -> 30%
where the time goes in v3:
time: 228 us; the launch traced here: 226 us
  Pallas kernels  189 us (83%)
  local copies, waits for them, and re-layouts  15.9 us (7%)
  starting transfers between devices  10.9 us (5%)
  other arithmetic  9.64 us (4%)
    pallas_call x1, Pallas kernels, transform(): pl.pallas_call(functools.partial(transform_kernel, lay), in_specs=[vmem]...  58.6 us
    pallas_call x1, Pallas kernels, sample(): pl.pallas_call(functools.partial(sample_kernel, lay), grid_spec=pltpu.Pre...  41 us
    pallas_call x1, Pallas kernels, spread(): pl.pallas_call(functools.partial(spread_kernel, lay), grid_spec=pltpu.Pre...  32.3 us
    pallas_call x1, Pallas kernels, gather_atoms(): pl.pallas_call(functools.partial(gather_kernel, lay), in_specs=[pl.BlockS...  27.5 us
    pallas_call x1, Pallas kernels, return_forces(): pl.pallas_call(functools.partial(return_kernel, lay), in_specs=[pl.BlockS...  17 us
    unnamed x28, local copies, waits for them, and re-layouts  12.6 us
    ppermute x4, starting transfers between devices, share_green(): messages.append(lax.ppermute(sent, ('row', 'col'), pairs))  9.51 us
    pallas_call x1, Pallas kernels, sort_atoms(): pl.pallas_call(functools.partial(sort_kernel, bins, lay.block_cols), grid...  7.76 us
  transfers between devices with their start and end apart: 5, of which 0 were waited for; matrix products, arithmetic and copies ran while one was open for 5% of the time, Pallas kernels for 30%

profile of v3, /device:TPU:0, one launch (start us, length us, event | category | flops | bytes accessed | tf_op | source)
XLA Modules:
  0.0 226.2 jit_solution(10032011076840273147)
XLA Ops:
  0.0 1.1 slice.89
  1.7 1.4 collective-permute-start
  4.2 0.8 compare_select_fusion.2
  5.0 0.8 copy.21
  5.9 0.9 fusion.10
  6.8 7.8 %sort_atoms.1 = (f32[2,8,2048]{2,1,0:T(8,128)S(1)}, f32[2,1,2048]{2,1,0:T(1,128)S(1)}) custom-call(f32[2,8,2048]{2,1,0:T(8,128)S(1)} %pad_maximum_fusion.2.payload_ref), custom_call_target="tpu_custom_call" | custom-call | tf_op jit(solution)/shard_map/sort_atoms/pallas_call | solution.py:162
  16.2 27.5 %gather_atoms.1.atoms_ref = f32[4,4,8,2048]{3,2,1,0:T(8,128)} custom-call(f32[2,8,2048]{2,1,0:T(8,128)} %copy-done.2), custom_call_target="tpu_custom_call" | custom-call | tf_op jit(solution)/shard_map/gather_atoms/pallas_call | solution.py:344
  43.8 2.5 %compare_select_fusion.1 = (f32[4,4,1,2048]{3,2,1,0:T(1,128)}, f32[4,4,1,2048]{3,2,1,0:T(1,128)S(1)}) fusion(f32[4,4,8,2048]{3,2,1,0:T(8,128)} %gather_atoms.1.atoms_ref), kind=kLoop, calls=%fused_computation.32 | loop fusion | flops 98304 | bytes 524288 | tf_op jit(solution)/shard_map/jit(_where)/select_n | solution.py:1029
  47.2 0.9 fusion.1
  48.1 0.9 fusion
  49.6 3.9 %collective-permute-start.4 = (f32[9,64,256]{2,1,0:T(8,128)S(1)}, f32[9,64,256]{2,1,0:T(8,128)S(1)}, u32[]{:S(2)}, u32[]{:S(2)}) collective-permute-start(f32[9,64,256]{2,1,0:T(8,128)S(1)} %get-tuple-element.37), channel_id=1, source_target_pairs={{0,17},{1,25},{2,19},{3,27},{4,21},{5,29},{6,23},{7,31},{8,1},{9,9... | collective-permute-start | bytes 1769480 | tf_op jit(solution)/shard_map/ppermute | solution.py:995
  53.5 1.9 collective-permute-start.3
  55.5 3.0 %collective-permute-start.2 = (f32[9,64,256]{2,1,0:T(8,128)S(1)}, f32[9,64,256]{2,1,0:T(8,128)S(1)}, u32[]{:S(2)}, u32[]{:S(2)}) collective-permute-start(f32[9,64,256]{2,1,0:T(8,128)S(1)} %get-tuple-element.39), channel_id=1, source_target_pairs={{0,16},{1,24},{2,18},{3,26},{4,20},{5,28},{6,22},{7,30},{8,0},{9,8... | collective-permute-start | bytes 1769480 | tf_op jit(solution)/shard_map/ppermute | solution.py:995
  59.4 32.3 %spread.1.mesh_ref = f32[4,5016,128]{2,1,0:T(8,128)S(1)} custom-call(s32[256]{0:T(256)S(1)} %get-tuple-element.50.starts_ref, s32[256]{0:T(256)S(1)} %get-tuple-element.49.turns_ref, f32[4,4,8,2048]{3,2,1,0:T(8,128)S(1)} %copy-done, s32[16,128]{1,0:T(8,128)S(1)} %broadcast_in_dim.91.waves_ref, f32[16,128]{1,0:T(8,128)S(1)} %broadcast_in_dim.92.packed_ref, ...), custom_call_target="tpu_custom_call" | custom-call | flops 10000000000 | bytes 10000000 | tf_op jit(solution)/shard_map/spread/pallas_call | solution.py:552
  91.8 3.9 %copy-done.3 = f32[4,5016,128]{2,1,0:T(8,128)} copy-done((f32[4,5016,128]{2,1,0:T(8,128)}, f32[4,5016,128]{2,1,0:T(8,128)S(1)}, u32[]{:S(2)}) %copy-start.3) | copy-done | bytes 10272792
  95.7 0.8 copy-done.10
  97.4 58.6 %transform.1 = (bf16[4,4864,128]{2,1,0:T(8,128)(2,1)}, bf16[4,4864,128]{2,1,0:T(8,128)(2,1)}) custom-call(f32[4,5016,128]{2,1,0:T(8,128)} %copy-done.3, f32[9,64,256]{2,1,0:T(8,128)} %copy-done.12, f32[9,64,256]{2,1,0:T(8,128)} %copy-done.11, f32[9,64,256]{2,1,0:T(8,128)} %copy-done.10, f32[9,64,256]{2,1,0:T(8,128)} %copy-done.9, ...), custom_call_target="tpu_custom_call" | custom-call | flops 10000000000 | bytes 10000000 | tf_op jit(solution)/shard_map/transform/pallas_call | solution.py:881
  156.0 2.4 %copy-done.4 = bf16[4,4864,128]{2,1,0:T(8,128)(2,1)S(1)} copy-done((bf16[4,4864,128]{2,1,0:T(8,128)(2,1)S(1)}, bf16[4,4864,128]{2,1,0:T(8,128)(2,1)}, u32[]{:S(2)}) %copy-start.4) | copy-done | bytes 4980760
  158.4 2.4 %copy-done.5 = bf16[4,4864,128]{2,1,0:T(8,128)(2,1)S(1)} copy-done((bf16[4,4864,128]{2,1,0:T(8,128)(2,1)S(1)}, bf16[4,4864,128]{2,1,0:T(8,128)(2,1)}, u32[]{:S(2)}) %copy-start.5) | copy-done | bytes 4980760
  160.8 41.0 %sample.1.force_ref = f32[4,4,3,16,128]{4,3,2,1,0:T(8,128)S(1)} custom-call(s32[256]{0:T(256)S(1)} %get-tuple-element.50.starts_ref, s32[256]{0:T(256)S(1)} %get-tuple-element.49.turns_ref, f32[4,4,8,2048]{3,2,1,0:T(8,128)S(1)} %copy-done, s32[16,128]{1,0:T(8,128)S(1)} %broadcast_in_dim.91.waves_ref, f32[16,128]{1,0:T(8,128)S(1)} %broadcast_in_dim.92.packed_ref, ...), custom_call_target="tpu_custom_call" | custom-call | flops 10000000000 | bytes 10000000 | tf_op jit(solution)/shard_map/sample/pallas_call | solution.py:655
  201.8 0.7 copy-done.1
  202.6 17.0 %return_forces.1 = f32[2,8,3,16,128]{4,3,2,1,0:T(8,128)} custom-call(f32[4,4,3,16,128]{4,3,2,1,0:T(8,128)} %copy-done.1), custom_call_target="tpu_custom_call" | custom-call | tf_op jit(solution)/shard_map/return_forces/pallas_call | solution.py:430
  219.5 1.0 reduce_sum.9
  220.6 4.9 %unsort_forces.1 = f32[2,8,2048]{2,1,0:T(8,128)S(1)} custom-call(f32[2,1,2048]{2,1,0:T(1,128)S(1)} %get-tuple-element.33.rank_ref, f32[2,8,2048]{2,1,0:T(8,128)S(1)} %pad.13.force_ref), custom_call_target="tpu_custom_call" | custom-call | tf_op jit(solution)/shard_map/unsort_forces/pallas_call | solution.py:200
  (59 shorter events, 7.1 us)
Async XLA Ops:
  1.1 14.3 %copy-start.6 = (f32[64,32,256]{2,1,0:T(8,128)S(1)}, f32[64,32,256]{2,1,0:T(8,128)}, u32[]{:S(2)}) copy-start(f32[64,32,256]{2,1,0:T(8,128)} %param.17) | copy-start | bytes 6291460
  1.7 47.5 %collective-permute-start = (f32[64,256]{1,0:T(8,128)}, f32[64,256]{1,0:T(8,128)S(1)}, u32[]{:S(2)}, u32[]{:S(2)}) collective-permute-start(f32[64,256]{1,0:T(8,128)} %bitcast.32), channel_id=1, source_target_pairs={{4,0},{12,8},{20,16},{28,24}} | collective-permute-start | bytes 196616 | tf_op jit(solution)/shard_map/ppermute | solution.py:971
  14.6 1.0 copy-start.2
  48.1 0.9 copy-start.7
  49.3 10.0 %copy-start.8 = (f32[6,16]{1,0:T(8,128)S(1)}, f32[6,16]{1,0:T(8,128)}, u32[]{:S(2)}) copy-start(f32[6,16]{1,0:T(8,128)} %get-tuple-element.54) | copy-start | bytes 1156
  49.3 10.1 %copy-start = (f32[4,4,8,2048]{3,2,1,0:T(8,128)S(1)}, f32[4,4,8,2048]{3,2,1,0:T(8,128)}, u32[]{:S(2)}) copy-start(f32[4,4,8,2048]{3,2,1,0:T(8,128)} %gather_atoms.1.atoms_ref) | copy-start | bytes 3145732
  49.6 46.1 %collective-permute-start.4 = (f32[9,64,256]{2,1,0:T(8,128)S(1)}, f32[9,64,256]{2,1,0:T(8,128)S(1)}, u32[]{:S(2)}, u32[]{:S(2)}) collective-permute-start(f32[9,64,256]{2,1,0:T(8,128)S(1)} %get-tuple-element.37), channel_id=1, source_target_pairs={{0,17},{1,25},{2,19},{3,27},{4,21},{5,29},{6,23},{7,31},{8,1},{9,9... | collective-permute-start | bytes 1769480 | tf_op jit(solution)/shard_map/ppermute | solution.py:995
  53.5 42.1 %collective-permute-start.3 = (f32[9,64,256]{2,1,0:T(8,128)S(1)}, f32[9,64,256]{2,1,0:T(8,128)S(1)}, u32[]{:S(2)}, u32[]{:S(2)}) collective-permute-start(f32[9,64,256]{2,1,0:T(8,128)S(1)} %get-tuple-element.38), channel_id=1, source_target_pairs={{0,1},{1,9},{2,3},{3,11},{4,5},{5,13},{6,7},{7,15},{8,16},{9,24},{... | collective-permute-start | bytes 1769480 | tf_op jit(solution)/shard_map/ppermute | solution.py:995
  55.5 40.2 %collective-permute-start.2 = (f32[9,64,256]{2,1,0:T(8,128)S(1)}, f32[9,64,256]{2,1,0:T(8,128)S(1)}, u32[]{:S(2)}, u32[]{:S(2)}) collective-permute-start(f32[9,64,256]{2,1,0:T(8,128)S(1)} %get-tuple-element.39), channel_id=1, source_target_pairs={{0,16},{1,24},{2,18},{3,26},{4,20},{5,28},{6,22},{7,30},{8,0},{9,8... | collective-permute-start | bytes 1769480 | tf_op jit(solution)/shard_map/ppermute | solution.py:995
  58.4 37.3 %collective-permute-start.1 = (f32[9,64,256]{2,1,0:T(8,128)S(1)}, f32[9,64,256]{2,1,0:T(8,128)S(1)}, u32[]{:S(2)}, u32[]{:S(2)}) collective-permute-start(f32[9,64,256]{2,1,0:T(8,128)S(1)} %get-tuple-element.40), channel_id=1, source_target_pairs={{0,0},{1,8},{2,2},{3,10},{4,4},{5,12},{6,6},{7,14},{8,17},{9,25},{... | collective-permute-start | bytes 1769480 | tf_op jit(solution)/shard_map/ppermute | solution.py:995
  91.8 3.9 %copy-start.3 = (f32[4,5016,128]{2,1,0:T(8,128)}, f32[4,5016,128]{2,1,0:T(8,128)S(1)}, u32[]{:S(2)}) copy-start(f32[4,5016,128]{2,1,0:T(8,128)S(1)} %spread.1.mesh_ref) | copy-start | bytes 30818308
  95.7 1.7 copy-start.9
  95.7 0.9 copy-start.10
  95.7 1.0 copy-start.11
  96.6 0.8 copy-start.12
  156.0 2.4 %copy-start.4 = (bf16[4,4864,128]{2,1,0:T(8,128)(2,1)S(1)}, bf16[4,4864,128]{2,1,0:T(8,128)(2,1)}, u32[]{:S(2)}) copy-start(bf16[4,4864,128]{2,1,0:T(8,128)(2,1)} %get-tuple-element.35.high_ref) | copy-start | bytes 14942212
  158.4 2.4 %copy-start.5 = (bf16[4,4864,128]{2,1,0:T(8,128)(2,1)S(1)}, bf16[4,4864,128]{2,1,0:T(8,128)(2,1)}, u32[]{:S(2)}) copy-start(bf16[4,4864,128]{2,1,0:T(8,128)(2,1)} %get-tuple-element.36.low_ref) | copy-start | bytes 14942212
  201.8 0.8 copy-start.1

commit v4 on v3

--- a/solution.py
+++ b/solution.py
@@ -696,6 +696,9 @@
         back_sem,
         home_sem,
         green_sem,
+        high_ref,
+        low_ref,
+        out_sem,
     ) = refs[lay.rows :]
     row = lax.axis_index("row")
     col = lax.axis_index("col")
@@ -853,16 +856,32 @@
         push_back(i).wait_recv()
         last(i, home_ref, i)
 
-    @pl.loop(0, lay.lines_padded)
-    def split(line):
-        where = pl.ds(pl.multiple_of(line * lay.wave_rows, lay.wave_rows), lay.wave_rows)
-        for r in range(lay.rows):
-            value = field_ref[r, pl.ds(line * lay.stride, lay.wave_rows), :]
-            out_high[r, where, :], out_low[r, where, :] = halves_of(value)
+    def leave(r):
+        return (
+            pltpu.make_async_copy(high_ref.at[r], out_high.at[r], out_sem.at[0, r]),
+            pltpu.make_async_copy(low_ref.at[r], out_low.at[r], out_sem.at[1, r]),
+        )
+
+    for r in range(lay.rows):
+
+        @pl.loop(0, lay.lines_padded, step=8)
+        def split(base):
+            for line in range(8):
+                first = pl.multiple_of((base + line) * lay.wave_rows, lay.wave_rows)
+                where = pl.ds(first, lay.wave_rows)
+                value = field_ref[r, pl.ds((base + line) * lay.stride, lay.wave_rows), :]
+                high_ref[r, where, :], low_ref[r, where, :] = halves_of(value)
+
+        for copy in leave(r):
+            copy.start()
 
     @pl.loop(0, own)
     def returned(i):
         push_back(i).wait_send()
+
+    for r in range(lay.rows):
+        for copy in leave(r):
+            copy.wait()
 
 
 def message_number(lay, row, col):
@@ -881,7 +900,7 @@
     return pl.pallas_call(
         functools.partial(transform_kernel, lay),
         in_specs=[vmem] + [pl.BlockSpec(memory_space=pl.ANY)] * lay.rows + [vmem] * len(tables),
-        out_specs=[vmem, vmem],
+        out_specs=[pl.BlockSpec(memory_space=pltpu.HBM)] * 2,
         out_shape=[out, out],
         scratch_shapes=[
             pltpu.VMEM(mesh.shape, jnp.float32),
@@ -896,6 +915,9 @@
             dma((lay.own,)),
             dma((lay.own,)),
             dma((lay.rows,)),
+            pltpu.VMEM(out.shape, jnp.bfloat16),
+            pltpu.VMEM(out.shape, jnp.bfloat16),
+            dma((2, lay.rows)),
         ],
         compiler_params=pltpu.CompilerParams(
             has_side_effects=True, vmem_limit_bytes=62 * 1024 * 1024

time: 228 us -> 226 us (level)
  no operation moved by 1% of the time
where the time goes in v4:
time: 226 us; the launch traced here: 225 us
  Pallas kernels  188 us (83%)
  local copies, waits for them, and re-layouts  15.9 us (7%)
  starting transfers between devices  10.9 us (5%)
  other arithmetic  9.64 us (4%)
    pallas_call x1, Pallas kernels, transform(): pl.pallas_call(functools.partial(transform_kernel, lay), in_specs=[vmem]...  57.1 us
    pallas_call x1, Pallas kernels, sample(): pl.pallas_call(functools.partial(sample_kernel, lay), grid_spec=pltpu.Pre...  41 us
    pallas_call x1, Pallas kernels, spread(): pl.pallas_call(functools.partial(spread_kernel, lay), grid_spec=pltpu.Pre...  32.3 us
    pallas_call x1, Pallas kernels, gather_atoms(): pl.pallas_call(functools.partial(gather_kernel, lay), in_specs=[pl.BlockS...  27.5 us
    pallas_call x1, Pallas kernels, return_forces(): pl.pallas_call(functools.partial(return_kernel, lay), in_specs=[pl.BlockS...  17 us
    unnamed x28, local copies, waits for them, and re-layouts  12.6 us
    ppermute x4, starting transfers between devices, share_green(): messages.append(lax.ppermute(sent, ('row', 'col'), pairs))  9.51 us
    pallas_call x1, Pallas kernels, sort_atoms(): pl.pallas_call(functools.partial(sort_kernel, bins, lay.block_cols), grid...  7.76 us
  transfers between devices with their start and end apart: 5, of which 0 were waited for; matrix products, arithmetic and copies ran while one was open for 5% of the time, Pallas kernels for 30%

profile of v4, /device:TPU:0, one launch (start us, length us, event | category | flops | bytes accessed | tf_op | source)
XLA Modules:
  0.0 224.6 jit_solution(3712424145143831997)
XLA Ops:
  0.0 1.1 slice.89
  1.7 1.4 collective-permute-start
  4.2 0.8 compare_select_fusion.2
  5.0 0.8 copy.21
  5.9 0.9 fusion.10
  6.8 7.8 %sort_atoms.1 = (f32[2,8,2048]{2,1,0:T(8,128)S(1)}, f32[2,1,2048]{2,1,0:T(1,128)S(1)}) custom-call(f32[2,8,2048]{2,1,0:T(8,128)S(1)} %pad_maximum_fusion.2.payload_ref), custom_call_target="tpu_custom_call" | custom-call | tf_op jit(solution)/shard_map/sort_atoms/pallas_call | solution.py:162
  16.2 27.5 %gather_atoms.1.atoms_ref = f32[4,4,8,2048]{3,2,1,0:T(8,128)} custom-call(f32[2,8,2048]{2,1,0:T(8,128)} %copy-done.2), custom_call_target="tpu_custom_call" | custom-call | tf_op jit(solution)/shard_map/gather_atoms/pallas_call | solution.py:344
  43.8 2.5 %compare_select_fusion.1 = (f32[4,4,1,2048]{3,2,1,0:T(1,128)}, f32[4,4,1,2048]{3,2,1,0:T(1,128)S(1)}) fusion(f32[4,4,8,2048]{3,2,1,0:T(8,128)} %gather_atoms.1.atoms_ref), kind=kLoop, calls=%fused_computation.32 | loop fusion | flops 98304 | bytes 524288 | tf_op jit(solution)/shard_map/jit(_where)/select_n | solution.py:1051
  47.2 0.9 fusion.1
  48.1 0.9 fusion
  49.6 3.9 %collective-permute-start.4 = (f32[9,64,256]{2,1,0:T(8,128)S(1)}, f32[9,64,256]{2,1,0:T(8,128)S(1)}, u32[]{:S(2)}, u32[]{:S(2)}) collective-permute-start(f32[9,64,256]{2,1,0:T(8,128)S(1)} %get-tuple-element.37), channel_id=1, source_target_pairs={{0,17},{1,25},{2,19},{3,27},{4,21},{5,29},{6,23},{7,31},{8,1},{9,9... | collective-permute-start | bytes 1769480 | tf_op jit(solution)/shard_map/ppermute | solution.py:1017
  53.5 1.9 collective-permute-start.3
  55.5 3.0 %collective-permute-start.2 = (f32[9,64,256]{2,1,0:T(8,128)S(1)}, f32[9,64,256]{2,1,0:T(8,128)S(1)}, u32[]{:S(2)}, u32[]{:S(2)}) collective-permute-start(f32[9,64,256]{2,1,0:T(8,128)S(1)} %get-tuple-element.39), channel_id=1, source_target_pairs={{0,16},{1,24},{2,18},{3,26},{4,20},{5,28},{6,22},{7,30},{8,0},{9,8... | collective-permute-start | bytes 1769480 | tf_op jit(solution)/shard_map/ppermute | solution.py:1017
  59.4 32.3 %spread.1.mesh_ref = f32[4,5016,128]{2,1,0:T(8,128)S(1)} custom-call(s32[256]{0:T(256)S(1)} %get-tuple-element.50.starts_ref, s32[256]{0:T(256)S(1)} %get-tuple-element.49.turns_ref, f32[4,4,8,2048]{3,2,1,0:T(8,128)S(1)} %copy-done, s32[16,128]{1,0:T(8,128)S(1)} %broadcast_in_dim.91.waves_ref, f32[16,128]{1,0:T(8,128)S(1)} %broadcast_in_dim.92.packed_ref, ...), custom_call_target="tpu_custom_call" | custom-call | flops 10000000000 | bytes 10000000 | tf_op jit(solution)/shard_map/spread/pallas_call | solution.py:552
  91.8 3.9 %copy-done.3 = f32[4,5016,128]{2,1,0:T(8,128)} copy-done((f32[4,5016,128]{2,1,0:T(8,128)}, f32[4,5016,128]{2,1,0:T(8,128)S(1)}, u32[]{:S(2)}) %copy-start.3) | copy-done | bytes 10272792
  95.7 0.8 copy-done.10
  97.4 57.1 %transform.1 = (bf16[4,4864,128]{2,1,0:T(8,128)(2,1)}, bf16[4,4864,128]{2,1,0:T(8,128)(2,1)}) custom-call(f32[4,5016,128]{2,1,0:T(8,128)} %copy-done.3, f32[9,64,256]{2,1,0:T(8,128)} %copy-done.12, f32[9,64,256]{2,1,0:T(8,128)} %copy-done.11, f32[9,64,256]{2,1,0:T(8,128)} %copy-done.10, f32[9,64,256]{2,1,0:T(8,128)} %copy-done.9, ...), custom_call_target="tpu_custom_call" | custom-call | flops 10000000000 | bytes 10000000 | tf_op jit(solution)/shard_map/transform/pallas_call | solution.py:900
  154.5 2.4 %copy-done.4 = bf16[4,4864,128]{2,1,0:T(8,128)(2,1)S(1)} copy-done((bf16[4,4864,128]{2,1,0:T(8,128)(2,1)S(1)}, bf16[4,4864,128]{2,1,0:T(8,128)(2,1)}, u32[]{:S(2)}) %copy-start.4) | copy-done | bytes 4980760
  156.9 2.4 %copy-done.5 = bf16[4,4864,128]{2,1,0:T(8,128)(2,1)S(1)} copy-done((bf16[4,4864,128]{2,1,0:T(8,128)(2,1)S(1)}, bf16[4,4864,128]{2,1,0:T(8,128)(2,1)}, u32[]{:S(2)}) %copy-start.5) | copy-done | bytes 4980760
  159.3 41.0 %sample.1.force_ref = f32[4,4,3,16,128]{4,3,2,1,0:T(8,128)S(1)} custom-call(s32[256]{0:T(256)S(1)} %get-tuple-element.50.starts_ref, s32[256]{0:T(256)S(1)} %get-tuple-element.49.turns_ref, f32[4,4,8,2048]{3,2,1,0:T(8,128)S(1)} %copy-done, s32[16,128]{1,0:T(8,128)S(1)} %broadcast_in_dim.91.waves_ref, f32[16,128]{1,0:T(8,128)S(1)} %broadcast_in_dim.92.packed_ref, ...), custom_call_target="tpu_custom_call" | custom-call | flops 10000000000 | bytes 10000000 | tf_op jit(solution)/shard_map/sample/pallas_call | solution.py:655
  200.3 0.7 copy-done.1
  201.0 17.0 %return_forces.1 = f32[2,8,3,16,128]{4,3,2,1,0:T(8,128)} custom-call(f32[4,4,3,16,128]{4,3,2,1,0:T(8,128)} %copy-done.1), custom_call_target="tpu_custom_call" | custom-call | tf_op jit(solution)/shard_map/return_forces/pallas_call | solution.py:430
  218.0 1.0 reduce_sum.9
  219.1 4.9 %unsort_forces.1 = f32[2,8,2048]{2,1,0:T(8,128)S(1)} custom-call(f32[2,1,2048]{2,1,0:T(1,128)S(1)} %get-tuple-element.33.rank_ref, f32[2,8,2048]{2,1,0:T(8,128)S(1)} %pad.13.force_ref), custom_call_target="tpu_custom_call" | custom-call | tf_op jit(solution)/shard_map/unsort_forces/pallas_call | solution.py:200
  (59 shorter events, 7.1 us)
Async XLA Ops:
  1.1 14.3 %copy-start.6 = (f32[64,32,256]{2,1,0:T(8,128)S(1)}, f32[64,32,256]{2,1,0:T(8,128)}, u32[]{:S(2)}) copy-start(f32[64,32,256]{2,1,0:T(8,128)} %param.17) | copy-start | bytes 6291460
  1.7 47.5 %collective-permute-start = (f32[64,256]{1,0:T(8,128)}, f32[64,256]{1,0:T(8,128)S(1)}, u32[]{:S(2)}, u32[]{:S(2)}) collective-permute-start(f32[64,256]{1,0:T(8,128)} %bitcast.32), channel_id=1, source_target_pairs={{4,0},{12,8},{20,16},{28,24}} | collective-permute-start | bytes 196616 | tf_op jit(solution)/shard_map/ppermute | solution.py:993
  14.6 1.0 copy-start.2
  48.1 0.9 copy-start.7
  49.3 10.0 %copy-start.8 = (f32[6,16]{1,0:T(8,128)S(1)}, f32[6,16]{1,0:T(8,128)}, u32[]{:S(2)}) copy-start(f32[6,16]{1,0:T(8,128)} %get-tuple-element.54) | copy-start | bytes 1156
  49.3 10.1 %copy-start = (f32[4,4,8,2048]{3,2,1,0:T(8,128)S(1)}, f32[4,4,8,2048]{3,2,1,0:T(8,128)}, u32[]{:S(2)}) copy-start(f32[4,4,8,2048]{3,2,1,0:T(8,128)} %gather_atoms.1.atoms_ref) | copy-start | bytes 3145732
  49.6 46.1 %collective-permute-start.4 = (f32[9,64,256]{2,1,0:T(8,128)S(1)}, f32[9,64,256]{2,1,0:T(8,128)S(1)}, u32[]{:S(2)}, u32[]{:S(2)}) collective-permute-start(f32[9,64,256]{2,1,0:T(8,128)S(1)} %get-tuple-element.37), channel_id=1, source_target_pairs={{0,17},{1,25},{2,19},{3,27},{4,21},{5,29},{6,23},{7,31},{8,1},{9,9... | collective-permute-start | bytes 1769480 | tf_op jit(solution)/shard_map/ppermute | solution.py:1017
  53.5 42.1 %collective-permute-start.3 = (f32[9,64,256]{2,1,0:T(8,128)S(1)}, f32[9,64,256]{2,1,0:T(8,128)S(1)}, u32[]{:S(2)}, u32[]{:S(2)}) collective-permute-start(f32[9,64,256]{2,1,0:T(8,128)S(1)} %get-tuple-element.38), channel_id=1, source_target_pairs={{0,1},{1,9},{2,3},{3,11},{4,5},{5,13},{6,7},{7,15},{8,16},{9,24},{... | collective-permute-start | bytes 1769480 | tf_op jit(solution)/shard_map/ppermute | solution.py:1017
  55.5 40.2 %collective-permute-start.2 = (f32[9,64,256]{2,1,0:T(8,128)S(1)}, f32[9,64,256]{2,1,0:T(8,128)S(1)}, u32[]{:S(2)}, u32[]{:S(2)}) collective-permute-start(f32[9,64,256]{2,1,0:T(8,128)S(1)} %get-tuple-element.39), channel_id=1, source_target_pairs={{0,16},{1,24},{2,18},{3,26},{4,20},{5,28},{6,22},{7,30},{8,0},{9,8... | collective-permute-start | bytes 1769480 | tf_op jit(solution)/shard_map/ppermute | solution.py:1017
  58.4 37.3 %collective-permute-start.1 = (f32[9,64,256]{2,1,0:T(8,128)S(1)}, f32[9,64,256]{2,1,0:T(8,128)S(1)}, u32[]{:S(2)}, u32[]{:S(2)}) collective-permute-start(f32[9,64,256]{2,1,0:T(8,128)S(1)} %get-tuple-element.40), channel_id=1, source_target_pairs={{0,0},{1,8},{2,2},{3,10},{4,4},{5,12},{6,6},{7,14},{8,17},{9,25},{... | collective-permute-start | bytes 1769480 | tf_op jit(solution)/shard_map/ppermute | solution.py:1017
  91.8 3.9 %copy-start.3 = (f32[4,5016,128]{2,1,0:T(8,128)}, f32[4,5016,128]{2,1,0:T(8,128)S(1)}, u32[]{:S(2)}) copy-start(f32[4,5016,128]{2,1,0:T(8,128)S(1)} %spread.1.mesh_ref) | copy-start | bytes 30818308
  95.7 1.7 copy-start.9
  95.7 0.9 copy-start.10
  95.7 1.0 copy-start.11
  96.6 0.8 copy-start.12
  154.5 2.4 %copy-start.4 = (bf16[4,4864,128]{2,1,0:T(8,128)(2,1)S(1)}, bf16[4,4864,128]{2,1,0:T(8,128)(2,1)}, u32[]{:S(2)}) copy-start(bf16[4,4864,128]{2,1,0:T(8,128)(2,1)} %get-tuple-element.35.high_ref) | copy-start | bytes 14942212
  156.9 2.4 %copy-start.5 = (bf16[4,4864,128]{2,1,0:T(8,128)(2,1)S(1)}, bf16[4,4864,128]{2,1,0:T(8,128)(2,1)}, u32[]{:S(2)}) copy-start(bf16[4,4864,128]{2,1,0:T(8,128)(2,1)} %get-tuple-element.36.low_ref) | copy-start | bytes 14942212
  200.2 0.8 copy-start.1
